TPU v7x, 8 devices: a whole 2x2x1 slice. The times are simulated.
8 devices in a mesh: tp: 4 (over z, y, x), pool: 2 (over core).
Axes of the slice: x: 2, y: 2, z: 1, core: 2. Of those that a mesh axis runs over, the one named last changes fastest.
Arguments:
- base_up: bfloat16 [1, 8192, 32768], P(None, None, 'tp')
- base_down: bfloat16 [1, 32768, 8192], P(None, 'tp')
- up_left: float32 [2, 1, 8192, 128], P('pool', None, 'tp')
- up_right: float32 [2, 1, 128, 32768], P('pool', None, None, 'tp')
- down_left: float32 [2, 1, 32768, 128], P('pool', None, 'tp')
- down_right: float32 [2, 1, 128, 8192], P('pool', None, None, 'tp')
- grad_up_left: float32 [2, 1, 8192, 128], P('pool', None, 'tp')
- grad_up_right: float32 [2, 1, 128, 32768], P('pool', None, None, 'tp')
- grad_down_left: float32 [2, 1, 32768, 128], P('pool', None, 'tp')
- grad_down_right: float32 [2, 1, 128, 8192], P('pool', None, None, 'tp')
- learn_rate: float32 [1], replicated
- prompts: bfloat16 [2, 2048, 8192], P('pool')
Outputs:
- output 1: float32 [2, 1, 8192, 128], P('pool', None, 'tp')
- output 2: float32 [2, 1, 128, 32768], P('pool', None, None, 'tp')
- output 3: float32 [2, 1, 32768, 128], P('pool', None, 'tp')
- output 4: float32 [2, 1, 128, 8192], P('pool', None, None, 'tp')
- output 5: bfloat16 [2, 2048, 8192], P('pool')
All inputs are finite; a program needn't handle non-finite values.
Results may differ from a plain program's by a relative error of at most 0.00188.
Values are sent between devices in bfloat16 or wider.
A program may use at most 1.5 GiB of HBM per device.

v0:
```python
import functools

import jax
import jax.numpy as jnp
from jax import lax
from jax.experimental import pallas as pl
from jax.experimental.pallas import tpu as pltpu
from jax.sharding import PartitionSpec as P

CHUNK = 512
TILE = 256
RING = 3
LAG = (2, 4, 7, 23)
BF16 = jnp.bfloat16
F32 = jnp.float32
MESH = pl.DeviceIdType.MESH


def mlp_kernel(dims, base_up, base_dn, a_up, b_up, a_dn, b_dn, prompts, hid, wm,
               x, u, wb, aup, bup, adn, bdn, pb, rx0, s1, rx1, rx2, ob, res,
               wsem, osem, lsem, asend, arecv, xsem, s0, r0, ss1, rs1, ss2, rs2, ss3, rs3, ss4, ss5, fsem,
               xfree, cr1, cr2, cr3):
    m, nc, nb, d, fh, w = dims
    total = nc * nb
    ring = nb
    halves = w // TILE
    mh, mq, me = m // 2, m // 4, m // 8
    d4 = d // 4
    t = lax.axis_index('tp')
    c = lax.axis_index('pool')
    xb, yb = t % 2, t // 2
    near_x, near_y = t + 1 - 2 * xb, t + 2 - 4 * yb
    b1 = (1 - c) * xb + c * yb
    b2 = c * xb + (1 - c) * yb
    p1 = (1 - c) * near_x + c * near_y
    p2 = c * near_x + (1 - c) * near_y

    def rows(start, size):
        return pl.ds(pl.multiple_of(start, size), size)

    def remote(src, dst, send, recv, device):
        return pltpu.make_async_remote_copy(src_ref=src, dst_ref=dst, send_sem=send, recv_sem=recv,
                                            device_id=device, device_id_type=MESH)

    def base_loads(r, slot):
        @pl.when(r < nb)
        def _():
            pltpu.make_async_copy(base_up.at[0, :, rows(c * fh + r * TILE, TILE)], wb.at[slot], wsem.at[slot]).start()

        @pl.when(r >= nb)
        def _():
            for h in range(halves):
                pltpu.make_async_copy(base_dn.at[0, rows(c * fh, fh), rows((r - nb) * w + h * TILE, TILE)],
                                      wb.at[slot, pl.ds(h * fh, fh), :], wsem.at[slot]).start()

    def merged_load(r, slot):
        return pltpu.make_async_copy(wm.at[r], wb.at[slot], wsem.at[slot])

    def merged_store(r, slot):
        return pltpu.make_async_copy(wb.at[slot], wm.at[r], osem.at[slot])

    piece = min(512, fh)

    def merge_up(slot, j):
        right = bup[:, rows(j * TILE, TILE)]
        for q in range(d // piece):
            part = pl.ds(q * piece, piece)
            delta = jnp.dot(aup[part, :], right, preferred_element_type=F32).astype(BF16)
            wb[slot, part, :] = wb[slot, part, :] + delta

    def merge_dn(slot, i):
        for h in range(halves):
            right = bdn[:, rows(i * w + h * TILE, TILE)]
            for q in range(fh // piece):
                delta = jnp.dot(adn[pl.ds(q * piece, piece), :], right, preferred_element_type=F32).astype(BF16)
                part = pl.ds(h * fh + q * piece, piece)
                wb[slot, part, :] = wb[slot, part, :] + delta

    def dot_up(slot, j):
        pre = jnp.dot(x[...], wb[slot], preferred_element_type=F32)
        u[:, rows(j * TILE, TILE)] = jax.nn.gelu(pre, approximate=True).astype(BF16)

    def dot_dn(slot, buf):
        for h in range(halves):
            pb[buf, :, pl.ds(h * TILE, TILE)] = jnp.dot(u[...], wb[slot, pl.ds(h * fh, fh), :],
                                                        preferred_element_type=F32)

    def swap(g):
        return remote(pb.at[g % 2, rows((1 - c) * mh, mh), :], rx0.at[g % 4], s0.at[g % 2], r0.at[g % 4], (t, 1 - c))

    def first(g):
        return remote(s1.at[g % ring, rows((1 - b1) * mq, mq), :], rx1.at[g % ring],
                      ss1.at[g % ring], rs1.at[g % ring], (p1, c))

    def second(g):
        return remote(s1.at[g % ring, rows(b1 * mq + (1 - b2) * me, me), :], rx2.at[g % ring],
                      ss2.at[g % ring], rs2.at[g % ring], (p2, c))

    def gather(g):
        half = ob.at[g % ring, rows(b2 * me, me), :]
        return remote(half, half, ss3.at[g % ring], rs3.at[g % ring], (p2, c))

    def final_place(g):
        return hid.at[rows((g // nb) * m + c * mh + b1 * mq, mq), rows((g % nb) * w, w)]

    def final_far(g):
        return remote(ob.at[g % ring], final_place(g), ss4.at[g % ring], fsem.at[1 + c], (p1, 1))

    def final_near(g):
        return remote(ob.at[g % ring], final_place(g), ss5.at[g % ring], fsem.at[0], (t, 1))

    def final_local(g):
        return pltpu.make_async_copy(ob.at[g % ring], final_place(g), ss5.at[g % ring])

    def stage_a(g):
        slot = g % ring
        swap(g).wait_send()
        swap(g).wait_recv()
        s1[slot] = pb[g % 2, rows(c * mh, mh), :] + rx0[g % 4]

        @pl.when(g >= ring)
        def _():
            pl.semaphore_wait(cr1, 1)
        first(g).start()

    def stage_b(g):
        slot = g % ring
        keep = rows(b1 * mq, mq)
        first(g).wait_recv()
        s1[slot, keep, :] = s1[slot, keep, :] + rx1[slot]

        @pl.when(g + ring < total)
        def _():
            pl.semaphore_signal(cr1, inc=1, device_id=(p1, c), device_id_type=MESH)

        @pl.when(g >= ring)
        def _():
            pl.semaphore_wait(cr2, 1)
        second(g).start()

    def stage_c(g):
        slot = g % ring
        keep = rows(b1 * mq + b2 * me, me)
        second(g).wait_recv()
        first(g).wait_send()
        held = res[(g // nb) % 2, :, rows((g % nb) * w, w)].astype(F32)
        ob[slot, rows(b2 * me, me), :] = (held + (s1[slot, keep, :] + rx2[slot])).astype(BF16)

        @pl.when(g + ring < total)
        def _():
            pl.semaphore_signal(cr2, inc=1, device_id=(p2, c), device_id_type=MESH)

        @pl.when(g >= ring)
        def _():
            pl.semaphore_wait(cr3, 1)
        gather(g).start()

    def stage_d(g):
        gather(g).wait_recv()
        second(g).wait_send()
        final_far(g).start()

        @pl.when(c == 0)
        def _():
            final_near(g).start()

        @pl.when(c == 1)
        def _():
            final_local(g).start()

    def stage_e(g):
        gather(g).wait_send()
        final_far(g).wait_send()

        @pl.when(c == 0)
        def _():
            final_near(g).wait_send()

        @pl.when(c == 1)
        def _():
            final_local(g).wait()

        @pl.when(g + ring < total)
        def _():
            pl.semaphore_signal(cr3, inc=1, device_id=(p2, c), device_id_type=MESH)

    def stages(s):
        before = s - 1
        r = before % (2 * nb)

        @pl.when((r >= nb) & (before < 2 * nb * nc))
        def _():
            stage_a((before // (2 * nb)) * nb + r - nb)
        for lag, stage in zip(LAG, (stage_b, stage_c, stage_d, stage_e)):
            late = s - nb - lag

            @pl.when((late >= 0) & (late % 2 == 0) & (late < 2 * total))
            def _():
                stage(late // 2)

    def x_load(k):
        return pltpu.make_async_copy(prompts.at[0, rows(k * m, m), :], x, xsem.at[0])

    def x_send():
        return remote(x, x, xsem.at[1], xsem.at[2], (t, 0))

    def keep_rows(k):
        res[k % 2] = x[rows(c * mh + b1 * mq + b2 * me, me), :]

    def up_piece(owner):
        return aup.at[rows(owner * d4, d4), :]

    def dn_piece(owner):
        return bdn.at[:, rows(owner * d4, d4)]

    others = (near_x, near_y, 3 - t)

    def up_out(n):
        return remote(a_up, up_piece(t), asend.at[n], arecv.at[t], (others[n], 0))

    def dn_out(n):
        return remote(b_dn, dn_piece(t), asend.at[3 + n], arecv.at[4 + t], (others[n], 0))

    def up_in(owner):
        return remote(up_piece(owner), up_piece(owner), asend.at[6], arecv.at[owner], (t, 1))

    def dn_in(owner):
        return remote(dn_piece(owner), dn_piece(owner), asend.at[7], arecv.at[4 + owner], (t, 1))

    def pass_up(n):
        return remote(up_piece(others[n]), up_piece(others[n]), asend.at[8 + n], arecv.at[others[n]], (t, 1))

    def pass_dn(n):
        return remote(dn_piece(others[n]), dn_piece(others[n]), asend.at[11 + n], arecv.at[4 + others[n]], (t, 1))

    own = (
        lambda: remote(a_up, up_piece(t), asend.at[14], arecv.at[t], (t, 1)),
        lambda: remote(b_up.at[:, pl.ds(fh, fh)], bup, asend.at[15], arecv.at[8], (t, 1)),
        lambda: remote(a_dn.at[pl.ds(fh, fh), :], adn, asend.at[16], arecv.at[9], (t, 1)),
        lambda: remote(b_dn, dn_piece(t), asend.at[17], arecv.at[4 + t], (t, 1)),
    )
    local = (
        lambda: pltpu.make_async_copy(a_up, up_piece(t), lsem.at[0]),
        lambda: pltpu.make_async_copy(b_up.at[:, pl.ds(0, fh)], bup, lsem.at[1]),
        lambda: pltpu.make_async_copy(a_dn.at[pl.ds(0, fh), :], adn, lsem.at[2]),
        lambda: pltpu.make_async_copy(b_dn, dn_piece(t), lsem.at[3]),
    )

    base_loads(0, 0)
    base_loads(1, 1)

    @pl.when(c == 0)
    def _():
        for n in range(3):
            up_out(n).start()
        for n in range(4):
            own[n]().start()
            local[n]().start()
        for n in range(3):
            dn_out(n).start()
        for n in range(3):
            up_in(others[n]).wait_recv()
            pass_up(n).start()
        local[0]().wait()
        local[1]().wait()
        x_send().wait_recv()

    @pl.when(c == 1)
    def _():
        x_load(0).start()
        x_load(0).wait()
        x_send().start()
        for owner in range(4):
            up_in(owner).wait_recv()
        own[1]().wait_recv()

    merged_load(0, 0).wait()
    merge_up(0, 0)
    keep_rows(0)

    def tile_turn(r):
        merged_store(r, r % RING).start()

        @pl.when(r >= 1)
        def _():
            merged_store(r - 1, (r + 2) % RING).wait()

        @pl.when(r + 2 < 2 * nb)
        def _():
            base_loads(r + 2, (r + 2) % RING)

        @pl.when(r + 2 >= 2 * nb)
        def _():
            merged_load(r + 2 - 2 * nb, (r + 2) % RING).start()

        merged_load(0, (r + 1) % RING).wait()

    def first_up(r, carry):
        @pl.when(r == nb // 2)
        def _():
            @pl.when(c == 0)
            def _():
                for n in range(3):
                    dn_in(others[n]).wait_recv()
                    pass_dn(n).start()
        tile_turn(r)
        merge_up((r + 1) % RING, r + 1)
        dot_up(r % RING, r)
        return carry

    lax.fori_loop(0, nb - 1, first_up, 0)

    @pl.when(c == 0)
    def _():
        for n in range(3):
            up_out(n).wait_send()
            dn_out(n).wait_send()
            pass_up(n).wait_send()
            pass_dn(n).wait_send()
        for n in range(4):
            own[n]().wait_send()
        local[2]().wait()
        local[3]().wait()

    @pl.when(c == 1)
    def _():
        for owner in range(4):
            dn_in(owner).wait_recv()
        own[2]().wait_recv()

    tile_turn(nb - 1)
    merge_dn(nb % RING, 0)
    dot_up((nb - 1) % RING, nb - 1)

    def x_turn(k, r):
        @pl.when((k + 1 < nc) & (c == 0) & (r == nb))
        def _():
            pl.semaphore_signal(xfree, inc=1, device_id=(t, 1), device_id_type=MESH)

        @pl.when((k + 1 < nc) & (c == 1) & (r == nb))
        def _():
            @pl.when(k >= 0)
            def _():
                x_send().wait_send()
            x_load(k + 1).start()

        @pl.when((k + 1 < nc) & (c == 1) & (r == nb + 2))
        def _():
            x_load(k + 1).wait()
            pl.semaphore_wait(xfree, 1)
            x_send().start()

        @pl.when((k >= 1) & (r == 0))
        def _():
            @pl.when(c == 0)
            def _():
                x_send().wait_recv()
            keep_rows(k)

    def first_dn(r, carry):
        x_turn(0, r)
        tile_turn(r)
        merge_dn((r + 1) % RING, r + 1 - nb)
        dot_dn(r % RING, r % 2)
        swap(r - nb).start()
        stages(r)
        return carry

    lax.fori_loop(nb, 2 * nb - 1, first_dn, 0)

    def step(s, carry):
        k, r = s // (2 * nb), s % (2 * nb)
        x_turn(k, r)

        @pl.when(s == 2 * nb - 1)
        def _():
            tile_turn(2 * nb - 1)

        @pl.when(s == 2 * nb)
        def _():
            merged_store(2 * nb - 1, (2 * nb - 1) % RING).wait()

        @pl.when(s >= 2 * nb)
        def _():
            @pl.when(s + 2 < 2 * nb * nc)
            def _():
                merged_load((s + 2) % (2 * nb), (s + 2) % RING).start()

            @pl.when(s + 1 < 2 * nb * nc)
            def _():
                merged_load(0, (s + 1) % RING).wait()

        @pl.when(r < nb)
        def _():
            dot_up(s % RING, r)

        @pl.when(r >= nb)
        def _():
            dot_dn(s % RING, s % 2)
            swap(k * nb + r - nb).start()
        stages(s)
        return carry

    lax.fori_loop(2 * nb - 1, 2 * nb * nc, step, 0)

    def drain(s, carry):
        stages(s)
        return carry

    lax.fori_loop(2 * nb * nc, 2 * (total - 1) + nb + LAG[-1] + 1, drain, 0)

    @pl.when(c == 1)
    def _():
        x_send().wait_send()
        for n in range(3):
            part = hid.at[pl.ds(0, nc * mq), :]
            pltpu.make_async_copy(part, part, fsem.at[n]).wait()


def fused_mlp(base_up, base_down, a_up, b_up, a_dn, b_dn, prompts):
    tokens, d = prompts.shape[1:]
    fh = base_up.shape[2] // 2
    nb = fh // TILE
    w = d // nb
    m = min(CHUNK, tokens)
    nc = tokens // m
    rank = a_up.shape[1]
    dims = (m, nc, nb, d, fh, w)
    dma = pltpu.SemaphoreType.DMA
    anywhere = pl.BlockSpec(memory_space=pl.ANY)
    hid, _ = pl.pallas_call(
        functools.partial(mlp_kernel, dims),
        out_shape=(jax.ShapeDtypeStruct((tokens, d), BF16), jax.ShapeDtypeStruct((2 * nb, d, TILE), BF16)),
        in_specs=[anywhere] * 7,
        out_specs=(anywhere, anywhere),
        scratch_shapes=[
            pltpu.VMEM((m, d), BF16),
            pltpu.VMEM((m, fh), BF16),
            pltpu.VMEM((RING, d, TILE), BF16),
            pltpu.VMEM((d, rank), BF16),
            pltpu.VMEM((rank, fh), BF16),
            pltpu.VMEM((fh, rank), BF16),
            pltpu.VMEM((rank, d), BF16),
            pltpu.VMEM((2, m, w), F32),
            pltpu.VMEM((4, m // 2, w), F32),
            pltpu.VMEM((nb, m // 2, w), F32),
            pltpu.VMEM((nb, m // 4, w), F32),
            pltpu.VMEM((nb, m // 8, w), F32),
            pltpu.VMEM((nb, m // 4, w), BF16),
            pltpu.VMEM((2, m // 8, d), BF16),
            dma((RING,)), dma((RING,)), dma((4,)), dma((18,)), dma((10,)), dma((3,)),
            dma((2,)), dma((4,)), dma((nb,)), dma((nb,)), dma((nb,)), dma((nb,)), dma((nb,)), dma((nb,)),
            dma((nb,)), dma((nb,)), dma((3,)),
            pltpu.SemaphoreType.REGULAR, pltpu.SemaphoreType.REGULAR,
            pltpu.SemaphoreType.REGULAR, pltpu.SemaphoreType.REGULAR,
        ],
        compiler_params=pltpu.CompilerParams(has_side_effects=True, vmem_limit_bytes=67043328),
        name='mlp_ring',
    )(base_up, base_down, a_up, b_up, a_dn, b_dn, prompts)
    return hid


def solution(mesh):
    left_spec = P('pool', None, 'tp', None)
    right_spec = P('pool', None, None, 'tp')
    prompt_spec = P('pool', None, None)

    def local_step(base_up, base_down, up_left, up_right, down_left, down_right, grad_up_left, grad_up_right, grad_down_left, grad_down_right, learn_rate, prompts):
        step_size = learn_rate[0]
        new_up_left = up_left - step_size * grad_up_left
        new_up_right = up_right - step_size * grad_up_right
        new_down_left = down_left - step_size * grad_down_left
        new_down_right = down_right - step_size * grad_down_right
        own = tuple(part[0, 0].astype(BF16) for part in (new_up_left, new_up_right, new_down_left, new_down_right))
        hid = fused_mlp(base_up, base_down, *own, prompts)
        core = lax.axis_index('pool')
        hidden_out = jnp.where(core == 1, hid, jnp.zeros_like(hid))[None]
        return new_up_left, new_up_right, new_down_left, new_down_right, hidden_out

    return jax.shard_map(local_step, mesh=mesh,
                         in_specs=(P(None, None, 'tp'), P(None, 'tp', None), left_spec, right_spec, left_spec, right_spec, left_spec, right_spec, left_spec, right_spec, P(None), prompt_spec),
                         out_specs=(left_spec, right_spec, left_spec, right_spec, prompt_spec),
                         check_vma=False)
```

profile of v0, /device:TPU:1, one launch (start us, length us, event | category | flops | bytes accessed | tf_op | source)
XLA Modules:
  0.0 585.5 jit_solution(724525600988451562)
XLA Ops:
  1.3 2.8 convert_bitcast_fusion.3
  4.1 0.0 copy-start
  4.1 0.0 copy-start.1
  4.1 7.1 %convert_bitcast_fusion.1 = (bf16[128,8192]{1,0:T(8,128)(2,1)}, f32[1,1,128,8192]{3,2,1,0:T(8,128)}) fusion(f32[1,1,128,8192]{3,2,1,0:T(8,128)} %param.15, f32[1,1,128,8192]{3,2,1,0:T(8,128)} %param.19, f32[]{:T(128)} %bitcast.12), kind=kLoop, calls=%fused_computation.4 | loop fusion | flops 3145728 | bytes 14680068 | tf_op jit(solution)/shard_map/convert_element_type | solution.py:474
  11.2 0.0 copy-done
  11.2 0.4 copy-done.1
  11.6 0.0 copy-start.2
  11.6 0.0 copy-start.3
  11.6 3.3 convert_bitcast_fusion
  14.8 0.0 copy-done.2
  14.8 0.0 copy-done.3
  14.8 1.3 convert_bitcast_fusion.2
  16.1 546.5 %mlp_ring.1 = (bf16[2048,8192]{1,0:T(8,128)(2,1)}, bf16[32,8192,256]{2,1,0:T(8,128)(2,1)}) custom-call(bf16[1,8192,8192]{2,1,0:T(8,128)(2,1)} %base_up.1, bf16[1,8192,8192]{2,1,0:T(8,128)(2,1)} %base_dn.1, bf16[2048,128]{1,0:T(8,128)(2,1)} %get-tuple-element.13.a_up, bf16[128,8192]{1,0:T(8,128)(2,1)} %get-tuple-element.11.b_up, ...), custom_call_target="tpu_custom_call" | custom-call | tf_op jit(solution)/shard_map/mlp_ring/pallas_call | solution.py:431
  562.6 22.9 %select_bitcast_fusion = bf16[1,2048,8192]{2,1,0:T(8,128)(2,1)} fusion(bf16[2048,8192]{1,0:T(8,128)(2,1)} %get-tuple-element.6, pred[]{:T(512)S(6)} %eq.3), kind=kLoop, calls=%fused_computation | loop fusion | flops 16777216 | bytes 67108864 | tf_op jit(solution)/shard_map/broadcast_in_dim | solution.py:477
Async XLA Ops:
  4.1 7.1 %copy-start = (f32[1,1,8192,128]{3,2,1,0:T(8,128)S(1)}, f32[1,1,8192,128]{3,2,1,0:T(8,128)}, u32[]{:S(2)}) copy-start(f32[1,1,8192,128]{3,2,1,0:T(8,128)} %param.16) | copy-start | bytes 12582916
  4.1 7.5 %copy-start.1 = (f32[1,1,8192,128]{3,2,1,0:T(8,128)S(1)}, f32[1,1,8192,128]{3,2,1,0:T(8,128)}, u32[]{:S(2)}) copy-start(f32[1,1,8192,128]{3,2,1,0:T(8,128)} %param.20) | copy-start | bytes 12582916
  11.6 3.3 copy-start.2
  11.6 3.3 copy-start.3
where the time goes:
time: 586 us; the launch traced here: 585 us
  Pallas kernels  546 us (93%)
  other arithmetic  37.3 us (6%)
    pallas_call x1, Pallas kernels, fused_mlp(): pl.pallas_call(functools.partial(mlp_kernel, dims), out_shape=(jax.ShapeD...  546 us
    broadcast_in_dim x1, other arithmetic, local_step(): hidden_out = jnp.where(core == 1, hid, jnp.zeros_like(hid))[None]  22.9 us
    convert_element_type x4, other arithmetic, local_step(): part[0, 0].astype(BF16)  14.5 us

commit v1 on v0

--- a/solution.py
+++ b/solution.py
@@ -7,18 +7,18 @@
 from jax.experimental.pallas import tpu as pltpu
 from jax.sharding import PartitionSpec as P
 
-CHUNK = 512
+CHUNK = 256
 TILE = 256
 RING = 3
-LAG = (2, 4, 7, 23)
+LAG = (4, 7, 9, 25)
 BF16 = jnp.bfloat16
 F32 = jnp.float32
 MESH = pl.DeviceIdType.MESH
 
 
-def mlp_kernel(dims, base_up, base_dn, a_up, b_up, a_dn, b_dn, prompts, hid, wm,
-               x, u, wb, aup, bup, adn, bdn, pb, rx0, s1, rx1, rx2, ob, res,
-               wsem, osem, lsem, asend, arecv, xsem, s0, r0, ss1, rs1, ss2, rs2, ss3, rs3, ss4, ss5, fsem,
+def mlp_kernel(dims, base_up, base_dn, a_up, a_up_g, b_up, b_up_g, a_dn, a_dn_g, b_dn, b_dn_g, rate, prompts, hid, wm,
+               left, right, x, u, wb, aup, bup, adn, bdn, pb, rx0, s1, rx1, rx2, ob, res,
+               wsem, osem, lsem, rsem, asend, arecv, xsem, s0, r0, ss1, rs1, ss2, rs2, ss3, rs3, ss4, ss5, fsem,
                xfree, cr1, cr2, cr3):
     m, nc, nb, d, fh, w = dims
     total = nc * nb
@@ -26,6 +26,7 @@
     halves = w // TILE
     mh, mq, me = m // 2, m // 4, m // 8
     d4 = d // 4
+    rank = aup.shape[1]
     t = lax.axis_index('tp')
     c = lax.axis_index('pool')
     xb, yb = t % 2, t // 2
@@ -216,10 +217,10 @@
     others = (near_x, near_y, 3 - t)
 
     def up_out(n):
-        return remote(a_up, up_piece(t), asend.at[n], arecv.at[t], (others[n], 0))
+        return remote(up_piece(t), up_piece(t), asend.at[n], arecv.at[t], (others[n], 0))
 
     def dn_out(n):
-        return remote(b_dn, dn_piece(t), asend.at[3 + n], arecv.at[4 + t], (others[n], 0))
+        return remote(dn_piece(t), dn_piece(t), asend.at[3 + n], arecv.at[4 + t], (others[n], 0))
 
     def up_in(owner):
         return remote(up_piece(owner), up_piece(owner), asend.at[6], arecv.at[owner], (t, 1))
@@ -233,41 +234,91 @@
     def pass_dn(n):
         return remote(dn_piece(others[n]), dn_piece(others[n]), asend.at[11 + n], arecv.at[4 + others[n]], (t, 1))
 
+    far_b = u.at[pl.ds(0, rank), :]
+    far_a = wb.at[2, pl.ds(0, fh), pl.ds(0, rank)]
     own = (
-        lambda: remote(a_up, up_piece(t), asend.at[14], arecv.at[t], (t, 1)),
-        lambda: remote(b_up.at[:, pl.ds(fh, fh)], bup, asend.at[15], arecv.at[8], (t, 1)),
-        lambda: remote(a_dn.at[pl.ds(fh, fh), :], adn, asend.at[16], arecv.at[9], (t, 1)),
-        lambda: remote(b_dn, dn_piece(t), asend.at[17], arecv.at[4 + t], (t, 1)),
+        lambda: remote(up_piece(t), up_piece(t), asend.at[14], arecv.at[t], (t, 1)),
+        lambda: remote(far_b, bup, asend.at[15], arecv.at[8], (t, 1)),
+        lambda: remote(far_a, adn, asend.at[16], arecv.at[9], (t, 1)),
+        lambda: remote(dn_piece(t), dn_piece(t), asend.at[17], arecv.at[4 + t], (t, 1)),
     )
-    local = (
-        lambda: pltpu.make_async_copy(a_up, up_piece(t), lsem.at[0]),
-        lambda: pltpu.make_async_copy(b_up.at[:, pl.ds(0, fh)], bup, lsem.at[1]),
-        lambda: pltpu.make_async_copy(a_dn.at[pl.ds(0, fh), :], adn, lsem.at[2]),
-        lambda: pltpu.make_async_copy(b_dn, dn_piece(t), lsem.at[3]),
-    )
-
-    base_loads(0, 0)
-    base_loads(1, 1)
+
+    size = d4 // 2
+    lefts = [(a_up, a_up_g, q, aup, t * d4 + q * size) for q in range(2)]
+    lefts += [(a_dn, a_dn_g, q, adn, q * size) for q in range(4)]
+    lefts += [(a_dn, a_dn_g, 4 + q, None, q * size) for q in range(4)]
+    rights = [(b_up, b_up_g, q, bup, q * size) for q in range(4)]
+    rights += [(b_up, b_up_g, 4 + q, u, q * size) for q in range(4)]
+    rights += [(b_dn, b_dn_g, q, bdn, t * d4 + q * size) for q in range(2)]
+
+    def left_load(n):
+        value, grad, q, _, _ = lefts[n]
+        for side, src in enumerate((value, grad)):
+            pltpu.make_async_copy(src.at[0, 0, pl.ds(q * size, size), :], left.at[n % 2, side], lsem.at[n % 2]).start()
+
+    def right_load(n):
+        value, grad, q, _, _ = rights[n]
+        for side, src in enumerate((value, grad)):
+            pltpu.make_async_copy(src.at[0, 0, :, pl.ds(q * size, size)], right.at[n % 2, side], rsem.at[n % 2]).start()
+
+    def left_update(n):
+        _, _, _, dst, start = lefts[n]
+        pltpu.make_async_copy(left.at[n % 2], left.at[n % 2], lsem.at[n % 2]).wait()
+        new = (left[n % 2, 0] - rate[0] * left[n % 2, 1]).astype(BF16)
+        if dst is None:
+            wb[2, rows(start, size), pl.ds(0, rank)] = new
+        else:
+            dst[rows(start, size), :] = new
+        if n + 2 < len(lefts):
+            left_load(n + 2)
+
+    def right_update(n):
+        _, _, _, dst, start = rights[n]
+        pltpu.make_async_copy(right.at[n % 2], right.at[n % 2], rsem.at[n % 2]).wait()
+        new = (right[n % 2, 0] - rate[0] * right[n % 2, 1]).astype(BF16)
+        if dst is u:
+            u[pl.ds(0, rank), rows(start, size)] = new
+        else:
+            dst[:, rows(start, size)] = new
+        if n + 2 < len(rights):
+            right_load(n + 2)
 
     @pl.when(c == 0)
     def _():
+        for n in range(2):
+            left_load(n)
+        for n in range(2):
+            right_load(n)
+        base_loads(0, 0)
+        base_loads(1, 1)
+        for n in range(2):
+            left_update(n)
         for n in range(3):
             up_out(n).start()
-        for n in range(4):
-            own[n]().start()
-            local[n]().start()
+        own[0]().start()
+        for n in range(8):
+            right_update(n)
+        own[1]().start()
+        for n in range(8, 10):
+            right_update(n)
         for n in range(3):
             dn_out(n).start()
+        own[3]().start()
+        for n in range(2, 10):
+            left_update(n)
+        own[2]().start()
         for n in range(3):
             up_in(others[n]).wait_recv()
             pass_up(n).start()
-        local[0]().wait()
-        local[1]().wait()
+        own[1]().wait_send()
+        own[2]().wait_send()
         x_send().wait_recv()
 
     @pl.when(c == 1)
     def _():
         x_load(0).start()
+        base_loads(0, 0)
+        base_loads(1, 1)
         x_load(0).wait()
         x_send().start()
         for owner in range(4):
@@ -304,8 +355,11 @@
                     dn_in(others[n]).wait_recv()
                     pass_dn(n).start()
         tile_turn(r)
-        merge_up((r + 1) % RING, r + 1)
         dot_up(r % RING, r)
+
+        @pl.when(r < nb)
+        def _():
+            merge_up((r + 1) % RING, r + 1)
         return carry
 
     lax.fori_loop(0, nb - 1, first_up, 0)
@@ -317,10 +371,8 @@
             dn_out(n).wait_send()
             pass_up(n).wait_send()
             pass_dn(n).wait_send()
-        for n in range(4):
-            own[n]().wait_send()
-        local[2]().wait()
-        local[3]().wait()
+        own[0]().wait_send()
+        own[3]().wait_send()
 
     @pl.when(c == 1)
     def _():
@@ -360,8 +412,8 @@
     def first_dn(r, carry):
         x_turn(0, r)
         tile_turn(r)
+        dot_dn(r % RING, r % 2)
         merge_dn((r + 1) % RING, r + 1 - nb)
-        dot_dn(r % RING, r % 2)
         swap(r - nb).start()
         stages(r)
         return carry
@@ -417,23 +469,25 @@
             pltpu.make_async_copy(part, part, fsem.at[n]).wait()
 
 
-def fused_mlp(base_up, base_down, a_up, b_up, a_dn, b_dn, prompts):
+def fused_mlp(base_up, base_down, factors, learn_rate, prompts):
     tokens, d = prompts.shape[1:]
     fh = base_up.shape[2] // 2
     nb = fh // TILE
     w = d // nb
     m = min(CHUNK, tokens)
     nc = tokens // m
-    rank = a_up.shape[1]
+    rank = factors[0].shape[3]
     dims = (m, nc, nb, d, fh, w)
     dma = pltpu.SemaphoreType.DMA
     anywhere = pl.BlockSpec(memory_space=pl.ANY)
     hid, _ = pl.pallas_call(
         functools.partial(mlp_kernel, dims),
         out_shape=(jax.ShapeDtypeStruct((tokens, d), BF16), jax.ShapeDtypeStruct((2 * nb, d, TILE), BF16)),
-        in_specs=[anywhere] * 7,
+        in_specs=[anywhere] * 10 + [pl.BlockSpec(memory_space=pltpu.SMEM), anywhere],
         out_specs=(anywhere, anywhere),
         scratch_shapes=[
+            pltpu.VMEM((2, 2, d // 8, rank), F32),
+            pltpu.VMEM((2, 2, rank, d // 8), F32),
             pltpu.VMEM((m, d), BF16),
             pltpu.VMEM((m, fh), BF16),
             pltpu.VMEM((RING, d, TILE), BF16),
@@ -448,7 +502,7 @@
             pltpu.VMEM((nb, m // 8, w), F32),
             pltpu.VMEM((nb, m // 4, w), BF16),
             pltpu.VMEM((2, m // 8, d), BF16),
-            dma((RING,)), dma((RING,)), dma((4,)), dma((18,)), dma((10,)), dma((3,)),
+            dma((RING,)), dma((RING,)), dma((2,)), dma((2,)), dma((18,)), dma((10,)), dma((3,)),
             dma((2,)), dma((4,)), dma((nb,)), dma((nb,)), dma((nb,)), dma((nb,)), dma((nb,)), dma((nb,)),
             dma((nb,)), dma((nb,)), dma((3,)),
             pltpu.SemaphoreType.REGULAR, pltpu.SemaphoreType.REGULAR,
@@ -456,7 +510,7 @@
         ],
         compiler_params=pltpu.CompilerParams(has_side_effects=True, vmem_limit_bytes=67043328),
         name='mlp_ring',
-    )(base_up, base_down, a_up, b_up, a_dn, b_dn, prompts)
+    )(base_up, base_down, *factors, learn_rate, prompts)
     return hid
 
 
@@ -471,8 +525,8 @@
         new_up_right = up_right - step_size * grad_up_right
         new_down_left = down_left - step_size * grad_down_left
         new_down_right = down_right - step_size * grad_down_right
-        own = tuple(part[0, 0].astype(BF16) for part in (new_up_left, new_up_right, new_down_left, new_down_right))
-        hid = fused_mlp(base_up, base_down, *own, prompts)
+        factors = (up_left, grad_up_left, up_right, grad_up_right, down_left, grad_down_left, down_right, grad_down_right)
+        hid = fused_mlp(base_up, base_down, factors, learn_rate, prompts)
         core = lax.axis_index('pool')
         hidden_out = jnp.where(core == 1, hid, jnp.zeros_like(hid))[None]
         return new_up_left, new_up_right, new_down_left, new_down_right, hidden_out

time: 586 us -> 664 us (1.13); the launches traced: 585 us -> 657 us
  Pallas kernels: 546 us -> 620 us
    pallas_call x1, Pallas kernels: 546 us -> 620 us  [fused_mlp(): pl.pallas_call(functools.partial(mlp_kernel, dims), out_shape=(jax.ShapeD...]
    convert_element_type x4 -> x0, other arithmetic: 14.5 us -> none  [local_step(): part[0, 0].astype(BF16)]
    sub x0 -> x4, other arithmetic: none -> 10.9 us  [the longest x1 6.14 us: local_step(): new_down_left = down_left - step_size * grad_down_left]
where the time goes in v1:
time: 664 us; the launch traced here: 657 us
  Pallas kernels  620 us (93%)
  other arithmetic  33.8 us (5%)
    pallas_call x1, Pallas kernels, fused_mlp(): pl.pallas_call(functools.partial(mlp_kernel, dims), out_shape=(jax.ShapeD...  620 us
    broadcast_in_dim x1, other arithmetic, local_step(): hidden_out = jnp.where(core == 1, hid, jnp.zeros_like(hid))[None]  22.9 us

profile of v1, /device:TPU:1, one launch (start us, length us, event | category | flops | bytes accessed | tf_op | source)
XLA Modules:
  0.0 656.6 jit_solution(3307167992224411556)
XLA Ops:
  1.3 620.2 %mlp_ring.1 = (bf16[2048,8192]{1,0:T(8,128)(2,1)}, bf16[32,8192,256]{2,1,0:T(8,128)(2,1)}) custom-call(bf16[1,8192,8192]{2,1,0:T(8,128)(2,1)} %base_up.1, bf16[1,8192,8192]{2,1,0:T(8,128)(2,1)} %base_dn.1, f32[1,1,2048,128]{3,2,1,0:T(8,128)} %a_up.1, f32[1,1,2048,128]{3,2,1,0:T(8,128)} %a_up_g.1, f32[1,1,128,8192]{3,2,1,0:T(8,128)} %b_up.1, ...), custom_call_target="tpu_custom_call" | custom-call | tf_op jit(solution)/shard_map/mlp_ring/pallas_call | solution.py:483
  621.5 22.9 %select_bitcast_fusion = bf16[1,2048,8192]{2,1,0:T(8,128)(2,1)} fusion(bf16[2048,8192]{1,0:T(8,128)(2,1)} %get-tuple-element.6, pred[]{:T(512)S(6)} %eq.3), kind=kLoop, calls=%fused_computation | loop fusion | flops 16777216 | bytes 67108864 | tf_op jit(solution)/shard_map/broadcast_in_dim | solution.py:531
  644.4 0.0 copy-start
  644.4 0.0 copy-start.1
  644.4 6.1 multiply_subtract_fusion
  650.5 0.0 copy-done
  650.5 1.3 copy-done.1
  651.8 0.0 copy-start.2
  651.8 0.0 copy-start.3
  651.8 0.0 copy-start.4
  651.8 0.0 copy-start.5
  651.8 2.6 multiply_subtract_fusion.1
  654.4 0.0 copy-done.2
  654.4 0.0 copy-done.3
  654.4 1.1 multiply_subtract_fusion.2
  655.5 0.0 copy-done.4
  655.5 0.0 copy-done.5
  655.5 1.1 multiply_subtract_fusion.3
Async XLA Ops:
  644.4 6.2 copy-start
  644.4 7.4 %copy-start.1 = (f32[1,1,128,8192]{3,2,1,0:T(8,128)S(1)}, f32[1,1,128,8192]{3,2,1,0:T(8,128)}, u32[]{:S(2)}) copy-start(f32[1,1,128,8192]{3,2,1,0:T(8,128)} %b_up_g.1) | copy-start | bytes 12582916
  651.8 2.6 copy-start.2
  651.8 2.6 copy-start.3
  651.8 3.7 copy-start.4
  651.8 3.7 copy-start.5

commit v2 on v1

--- a/solution.py
+++ b/solution.py
@@ -7,16 +7,16 @@
 from jax.experimental.pallas import tpu as pltpu
 from jax.sharding import PartitionSpec as P
 
-CHUNK = 256
+CHUNK = 512
 TILE = 256
 RING = 3
-LAG = (4, 7, 9, 25)
+LAG = (2, 4, 7, 23)
 BF16 = jnp.bfloat16
 F32 = jnp.float32
 MESH = pl.DeviceIdType.MESH
 
 
-def mlp_kernel(dims, base_up, base_dn, a_up, a_up_g, b_up, b_up_g, a_dn, a_dn_g, b_dn, b_dn_g, rate, prompts, hid, wm,
+def mlp_kernel(dims, base_up, base_dn, a_up, a_up_g, b_up, b_up_g, a_dn, a_dn_g, b_dn, b_dn_g, rate, prompts, hid, tail, near, wm,
                left, right, x, u, wb, aup, bup, adn, bdn, pb, rx0, s1, rx1, rx2, ob, res,
                wsem, osem, lsem, rsem, asend, arecv, xsem, s0, r0, ss1, rs1, ss2, rs2, ss3, rs3, ss4, ss5, fsem,
                xfree, cr1, cr2, cr3):
@@ -156,30 +156,58 @@
             pl.semaphore_wait(cr3, 1)
         gather(g).start()
 
+    def tail_local(g):
+        return pltpu.make_async_copy(ob.at[g % ring], tail.at[:, rows((g % nb) * w, w)], ss4.at[g % ring])
+
+    def tail_near(g):
+        return remote(ob.at[g % ring], near.at[:, rows((g % nb) * w, w)], ss5.at[g % ring], fsem.at[3], (t, 1))
+
     def stage_d(g):
         gather(g).wait_recv()
         second(g).wait_send()
-        final_far(g).start()
-
-        @pl.when(c == 0)
-        def _():
-            final_near(g).start()
-
-        @pl.when(c == 1)
-        def _():
-            final_local(g).start()
+
+        @pl.when(g < total - nb)
+        def _():
+            final_far(g).start()
+
+            @pl.when(c == 0)
+            def _():
+                final_near(g).start()
+
+            @pl.when(c == 1)
+            def _():
+                final_local(g).start()
+
+        @pl.when(g >= total - nb)
+        def _():
+            tail_local(g).start()
+
+            @pl.when(c == 0)
+            def _():
+                tail_near(g).start()
 
     def stage_e(g):
         gather(g).wait_send()
-        final_far(g).wait_send()
-
-        @pl.when(c == 0)
-        def _():
-            final_near(g).wait_send()
-
-        @pl.when(c == 1)
-        def _():
-            final_local(g).wait()
+
+        @pl.when(g < total - nb)
+        def _():
+            final_far(g).wait_send()
+
+            @pl.when(c == 0)
+            def _():
+                final_near(g).wait_send()
+
+            @pl.when(c == 1)
+            def _():
+                final_local(g).wait()
+
+        @pl.when(g >= total - nb)
+        def _():
+            tail_local(g).wait()
+
+            @pl.when(c == 0)
+            def _():
+                tail_near(g).wait_send()
 
         @pl.when(g + ring < total)
         def _():
@@ -438,9 +466,9 @@
             def _():
                 merged_load((s + 2) % (2 * nb), (s + 2) % RING).start()
 
-            @pl.when(s + 1 < 2 * nb * nc)
-            def _():
-                merged_load(0, (s + 1) % RING).wait()
+            @pl.when(s > 2 * nb)
+            def _():
+                merged_load(0, s % RING).wait()
 
         @pl.when(r < nb)
         def _():
@@ -465,8 +493,9 @@
     def _():
         x_send().wait_send()
         for n in range(3):
-            part = hid.at[pl.ds(0, nc * mq), :]
+            part = hid.at[pl.ds(0, (nc - 1) * mq), :]
             pltpu.make_async_copy(part, part, fsem.at[n]).wait()
+        pltpu.make_async_copy(near, near, fsem.at[3]).wait()
 
 
 def fused_mlp(base_up, base_down, factors, learn_rate, prompts):
@@ -480,11 +509,12 @@
     dims = (m, nc, nb, d, fh, w)
     dma = pltpu.SemaphoreType.DMA
     anywhere = pl.BlockSpec(memory_space=pl.ANY)
-    hid, _ = pl.pallas_call(
+    hid, tail, near, _ = pl.pallas_call(
         functools.partial(mlp_kernel, dims),
-        out_shape=(jax.ShapeDtypeStruct((tokens, d), BF16), jax.ShapeDtypeStruct((2 * nb, d, TILE), BF16)),
+        out_shape=(jax.ShapeDtypeStruct((tokens, d), BF16), jax.ShapeDtypeStruct((m // 4, d), BF16),
+                   jax.ShapeDtypeStruct((m // 4, d), BF16), jax.ShapeDtypeStruct((2 * nb, d, TILE), BF16)),
         in_specs=[anywhere] * 10 + [pl.BlockSpec(memory_space=pltpu.SMEM), anywhere],
-        out_specs=(anywhere, anywhere),
+        out_specs=(anywhere,) * 4,
         scratch_shapes=[
             pltpu.VMEM((2, 2, d // 8, rank), F32),
             pltpu.VMEM((2, 2, rank, d // 8), F32),
@@ -504,14 +534,14 @@
             pltpu.VMEM((2, m // 8, d), BF16),
             dma((RING,)), dma((RING,)), dma((2,)), dma((2,)), dma((18,)), dma((10,)), dma((3,)),
             dma((2,)), dma((4,)), dma((nb,)), dma((nb,)), dma((nb,)), dma((nb,)), dma((nb,)), dma((nb,)),
-            dma((nb,)), dma((nb,)), dma((3,)),
+            dma((nb,)), dma((nb,)), dma((4,)),
             pltpu.SemaphoreType.REGULAR, pltpu.SemaphoreType.REGULAR,
             pltpu.SemaphoreType.REGULAR, pltpu.SemaphoreType.REGULAR,
         ],
         compiler_params=pltpu.CompilerParams(has_side_effects=True, vmem_limit_bytes=67043328),
         name='mlp_ring',
     )(base_up, base_down, *factors, learn_rate, prompts)
-    return hid
+    return hid, tail, near
 
 
 def solution(mesh):
@@ -521,14 +551,22 @@
 
     def local_step(base_up, base_down, up_left, up_right, down_left, down_right, grad_up_left, grad_up_right, grad_down_left, grad_down_right, learn_rate, prompts):
         step_size = learn_rate[0]
-        new_up_left = up_left - step_size * grad_up_left
-        new_up_right = up_right - step_size * grad_up_right
-        new_down_left = down_left - step_size * grad_down_left
-        new_down_right = down_right - step_size * grad_down_right
+        t, core = lax.axis_index('tp'), lax.axis_index('pool')
+        xb, yb = t % 2, t // 2
         factors = (up_left, grad_up_left, up_right, grad_up_right, down_left, grad_down_left, down_right, grad_down_right)
-        hid = fused_mlp(base_up, base_down, factors, learn_rate, prompts)
-        core = lax.axis_index('pool')
-        hidden_out = jnp.where(core == 1, hid, jnp.zeros_like(hid))[None]
+        hid, tail, near = fused_mlp(base_up, base_down, factors, learn_rate, prompts)
+        from_x = lax.ppermute(tail, ('tp', 'pool'), [(2 * n, 2 * (n ^ 1) + 1) for n in range(4)])
+        from_y = lax.ppermute(tail, ('tp', 'pool'), [(2 * n + 1, 2 * (n ^ 2) + 1) for n in range(4)])
+        trainer = core == 0
+        head = jnp.where(trainer, jnp.zeros_like(hid), hid)[None]
+        new = [jnp.where(trainer, value - step_size * grad, jnp.zeros_like(value))
+               for value, grad in zip(factors[::2], factors[1::2])]
+        new_up_left, new_up_right, new_down_left, new_down_right = new
+        last = jnp.concatenate([jnp.where(xb == 0, near, from_x), jnp.where(xb == 0, from_x, near),
+                                jnp.where(yb == 0, tail, from_y), jnp.where(yb == 0, from_y, tail)], axis=0)
+        last = jnp.where(trainer, jnp.zeros_like(last), last)[None]
+        head = lax.optimization_barrier(head)
+        hidden_out = lax.dynamic_update_slice(head, last, (0, hid.shape[0] - last.shape[1], 0))
         return new_up_left, new_up_right, new_down_left, new_down_right, hidden_out
 
     return jax.shard_map(local_step, mesh=mesh,

time: 664 us -> 552 us (0.83)
  Pallas kernels: 620 us -> 501 us
  other arithmetic: 33.8 us -> 41.4 us
    pallas_call x1, Pallas kernels: 620 us -> 501 us  [fused_mlp(): pl.pallas_call(functools.partial(mlp_kernel, dims), out_shape=(jax.ShapeD...]
    sub x4 -> x0, other arithmetic: 10.9 us -> none  [the longest x1 6.14 us: local_step(): new_down_left = down_left - step_size * grad_down_left]
    select_n x0 -> x4, other arithmetic: none -> 10.8 us  [local_step(): jnp.where(trainer, value - step_size * grad, jnp.zeros_like(value))]
  transfers between devices with their start and end apart: 0 -> 2, of which waited for: 0 -> 0; matrix products, arithmetic and copies ran while one was open for 0% -> 7% of each run, Pallas kernels for 0% -> 0%
where the time goes in v2:
time: 552 us; the launch traced here: 551 us
  Pallas kernels  501 us (91%)
  other arithmetic  41.4 us (8%)
  starting transfers between devices  5.75 us (1%)
    pallas_call x1, Pallas kernels, fused_mlp(): pl.pallas_call(functools.partial(mlp_kernel, dims), out_shape=(jax.ShapeD...  501 us
    broadcast_in_dim x1, other arithmetic, local_step(): head = jnp.where(trainer, jnp.zeros_like(hid), hid)[None]  22.9 us
  transfers between devices with their start and end apart: 2, of which 0 were waited for; matrix products, arithmetic and copies ran while one was open for 7% of the time, Pallas kernels for 0%

profile of v2, /device:TPU:1, one launch (start us, length us, event | category | flops | bytes accessed | tf_op | source)
XLA Modules:
  0.0 550.8 jit_solution(1233763687707451124)
XLA Ops:
  1.3 501.0 %mlp_ring.1 = (bf16[2048,8192]{1,0:T(8,128)(2,1)}, bf16[128,8192]{1,0:T(8,128)(2,1)}, bf16[128,8192]{1,0:T(8,128)(2,1)}, bf16[32,8192,256]{2,1,0:T(8,128)(2,1)}) custom-call(bf16[1,8192,8192]{2,1,0:T(8,128)(2,1)} %base_up.1, bf16[1,8192,8192]{2,1,0:T(8,128)(2,1)} %base_dn.1, f32[1,1,2048,128]{3,2,1,0:T(8,128)} %a_up.1, f32[1,1,2048,128]{3,2,1,0:T(8,128)} %a_up_g.1, ...), custom_call_target="tpu_custom_call" | custom-call | tf_op jit(solution)/shard_map/mlp_ring/pallas_call | solution.py:512
  502.3 1.3 collective-permute-start
  503.6 4.5 collective-permute-start.1
  508.0 22.9 %select_bitcast_fusion = bf16[1,2048,8192]{2,1,0:T(8,128)(2,1)} fusion(bf16[2048,8192]{1,0:T(8,128)(2,1)} %get-tuple-element.8, pred[]{:T(512)S(6)} %eq.13), kind=kLoop, calls=%fused_computation | loop fusion | flops 16777216 | bytes 67108864 | tf_op jit(solution)/shard_map/broadcast_in_dim | solution.py:561
  530.9 0.0 copy-start.2
  530.9 0.0 copy-start.3
  530.9 0.0 copy-start
  530.9 0.0 copy-start.1
  531.0 6.1 %subtract_select_fusion = f32[1,1,8192,128]{3,2,1,0:T(8,128)} fusion(f32[1,1,8192,128]{3,2,1,0:T(8,128)} %a_dn.1, f32[1,1,8192,128]{3,2,1,0:T(8,128)} %a_dn_g.1, f32[]{:T(128)} %bitcast.13, pred[]{:T(512)S(6)} %eq.13), kind=kLoop, calls=%fused_computation.3 | loop fusion | flops 3145728 | bytes 12582917 | tf_op jit(solution)/shard_map/jit(_where)/select_n | solution.py:562
  537.1 0.0 copy-done.2
  537.1 0.0 copy-done.3
  537.1 1.1 subtract_select_fusion.2
  538.2 0.0 copy-done
  538.2 1.1 copy-done.1
  539.3 0.0 copy-start.4
  539.3 0.0 copy-start.5
  539.3 2.5 subtract_select_fusion.1
  541.8 0.0 copy-done.4
  541.8 0.0 copy-done.5
  541.8 1.1 subtract_select_fusion.3
  542.9 0.0 copy-start.6
  542.9 0.0 collective-permute-done.1
  542.9 2.6 select_bitcast_fusion.2
  545.6 0.0 collective-permute-done
  545.6 0.2 copy-done.6
  545.8 0.5 select_bitcast_fusion.4
  546.3 4.5 fusion
Async XLA Ops:
  502.3 43.3 %collective-permute-start = (bf16[128,8192]{1,0:T(8,128)(2,1)}, bf16[128,8192]{1,0:T(8,128)(2,1)S(1)}, u32[]{:S(2)}, u32[]{:S(2)}) collective-permute-start(bf16[128,8192]{1,0:T(8,128)(2,1)} %get-tuple-element.10), channel_id=1, source_target_pairs={{0,3},{2,1},{4,7},{6,5}} | collective-permute-start | bytes 6291464 | tf_op jit(solution)/shard_map/ppermute | solution.py:558
  503.6 39.3 %collective-permute-start.1 = (bf16[128,8192]{1,0:T(8,128)(2,1)}, bf16[128,8192]{1,0:T(8,128)(2,1)}, u32[]{:S(2)}, u32[]{:S(2)}) collective-permute-start(bf16[128,8192]{1,0:T(8,128)(2,1)} %get-tuple-element.10), channel_id=1, source_target_pairs={{1,5},{3,7},{5,1},{7,3}} | collective-permute-start | bytes 6291464 | tf_op jit(solution)/shard_map/ppermute | solution.py:559
  530.9 6.2 %copy-start.2 = (f32[1,1,128,2048]{3,2,1,0:T(8,128)S(1)}, f32[1,1,128,2048]{3,2,1,0:T(8,128)}, u32[]{:S(2)}) copy-start(f32[1,1,128,2048]{3,2,1,0:T(8,128)} %b_dn.1) | copy-start | bytes 3145732
  530.9 6.2 %copy-start.3 = (f32[1,1,128,2048]{3,2,1,0:T(8,128)S(1)}, f32[1,1,128,2048]{3,2,1,0:T(8,128)}, u32[]{:S(2)}) copy-start(f32[1,1,128,2048]{3,2,1,0:T(8,128)} %b_dn_g.1) | copy-start | bytes 3145732
  530.9 7.3 %copy-start = (f32[1,1,128,8192]{3,2,1,0:T(8,128)S(1)}, f32[1,1,128,8192]{3,2,1,0:T(8,128)}, u32[]{:S(2)}) copy-start(f32[1,1,128,8192]{3,2,1,0:T(8,128)} %b_up.1) | copy-start | bytes 12582916
  530.9 8.4 %copy-start.1 = (f32[1,1,128,8192]{3,2,1,0:T(8,128)S(1)}, f32[1,1,128,8192]{3,2,1,0:T(8,128)}, u32[]{:S(2)}) copy-start(f32[1,1,128,8192]{3,2,1,0:T(8,128)} %b_up_g.1) | copy-start | bytes 12582916
  539.3 2.5 copy-start.4
  539.3 2.5 copy-start.5
  542.9 2.9 copy-start.6

commit v3 on v2

--- a/solution.py
+++ b/solution.py
@@ -544,29 +544,149 @@
     return hid, tail, near
 
 
+def finish_kernel(dims, hid, tail, near, a_up, a_up_g, b_up, b_up_g, a_dn, a_dn_g, b_dn, b_dn_g, rate,
+                  out, a_up_n, b_up_n, a_dn_n, b_dn_n, buf, left, right, left_n, right_n, isem, osem, lsem, rsem, lnsem, rnsem):
+    tokens, d, m, step = dims
+    t = lax.axis_index('tp')
+    c = lax.axis_index('pool')
+    xb, yb = t % 2, t // 2
+    mq = m // 4
+    head = tokens - m
+    slots = buf.shape[0]
+    ahead = slots // 2
+    size = d // 8
+
+    lefts = [(a_up, a_up_g, a_up_n, q) for q in range(2)] + [(a_dn, a_dn_g, a_dn_n, q) for q in range(8)]
+    rights = [(b_dn, b_dn_g, b_dn_n, q) for q in range(2)] + [(b_up, b_up_g, b_up_n, q) for q in range(8)]
+
+    def left_piece(ref, q):
+        return ref.at[0, 0, pl.ds(q * size, size), :]
+
+    def right_piece(ref, q):
+        return ref.at[0, 0, :, pl.ds(q * size, size)]
+
+    def left_store(n, slot):
+        return pltpu.make_async_copy(left_n.at[slot], left_piece(lefts[n][2], lefts[n][3]), lnsem.at[slot])
+
+    def right_store(n, slot):
+        return pltpu.make_async_copy(right_n.at[slot], right_piece(rights[n][2], rights[n][3]), rnsem.at[slot])
+
+    @pl.when(c == 1)
+    def _():
+        moves = [(hid, q * step, q * step) for q in range(head // step)]
+        moves += [(near, q * step, head + xb * mq + q * step) for q in range(mq // step)]
+        moves += [(tail, q * step, head + 2 * mq + yb * mq + q * step) for q in range(mq // step)]
+
+        def load(n):
+            src, start, _ = moves[n]
+            return pltpu.make_async_copy(src.at[pl.ds(start, step), :], buf.at[n % slots], isem.at[n % slots])
+
+        def store(n):
+            start = moves[n][2]
+            return pltpu.make_async_copy(buf.at[n % slots], out.at[0, pl.ds(pl.multiple_of(start, step), step), :], osem.at[n % slots])
+
+        for n in range(ahead):
+            load(n).start()
+        left_n[0] = jnp.zeros_like(left_n[0])
+        right_n[0] = jnp.zeros_like(right_n[0])
+        for n in range(len(moves)):
+            load(n).wait()
+            store(n).start()
+            if n < 10:
+                left_store(n, 0).start()
+                right_store(n, 0).start()
+            if n >= ahead:
+                store(n - ahead).wait()
+            if n + ahead < len(moves):
+                load(n + ahead).start()
+        for n in range(len(moves) - ahead, len(moves)):
+            store(n).wait()
+        for n in range(10):
+            left_store(n, 0).wait()
+            right_store(n, 0).wait()
+
+    @pl.when(c == 0)
+    def _():
+        def left_load(n):
+            for side in range(2):
+                pltpu.make_async_copy(left_piece(lefts[n][side], lefts[n][3]), left.at[n % 2, side], lsem.at[n % 2]).start()
+
+        def right_load(n):
+            for side in range(2):
+                pltpu.make_async_copy(right_piece(rights[n][side], rights[n][3]), right.at[n % 2, side], rsem.at[n % 2]).start()
+
+        def blank(n):
+            return pltpu.make_async_copy(buf.at[0], out.at[0, pl.ds(n * step, step), :], osem.at[0])
+
+        for n in range(2):
+            left_load(n)
+            right_load(n)
+        buf[0] = jnp.zeros_like(buf[0])
+        blanks = tokens // step
+        for n in range(10):
+            pltpu.make_async_copy(left.at[n % 2], left.at[n % 2], lsem.at[n % 2]).wait()
+            pltpu.make_async_copy(right.at[n % 2], right.at[n % 2], rsem.at[n % 2]).wait()
+            if n >= 2:
+                left_store(n - 2, n % 2).wait()
+                right_store(n - 2, n % 2).wait()
+            left_n[n % 2] = left[n % 2, 0] - rate[0] * left[n % 2, 1]
+            right_n[n % 2] = right[n % 2, 0] - rate[0] * right[n % 2, 1]
+            left_store(n, n % 2).start()
+            right_store(n, n % 2).start()
+            if n + 2 < 10:
+                left_load(n + 2)
+                right_load(n + 2)
+            for q in range(n * blanks // 10, (n + 1) * blanks // 10):
+                blank(q).start()
+        for n in range(8, 10):
+            left_store(n, n % 2).wait()
+            right_store(n, n % 2).wait()
+        for q in range(blanks):
+            blank(q).wait()
+
+
+def finish(hid, tail, near, factors, learn_rate, m):
+    tokens, d = hid.shape
+    rank = factors[0].shape[3]
+    step = min(64, m // 4)
+    dma = pltpu.SemaphoreType.DMA
+    anywhere = pl.BlockSpec(memory_space=pl.ANY)
+    return pl.pallas_call(
+        functools.partial(finish_kernel, (tokens, d, m, step)),
+        out_shape=(jax.ShapeDtypeStruct((1, tokens, d), BF16),) + tuple(jax.ShapeDtypeStruct(f.shape, F32) for f in factors[::2]),
+        in_specs=[anywhere] * 11 + [pl.BlockSpec(memory_space=pltpu.SMEM)],
+        out_specs=(anywhere,) * 5,
+        scratch_shapes=[
+            pltpu.VMEM((8, step, d), BF16),
+            pltpu.VMEM((2, 2, d // 8, rank), F32),
+            pltpu.VMEM((2, 2, rank, d // 8), F32),
+            pltpu.VMEM((2, d // 8, rank), F32),
+            pltpu.VMEM((2, rank, d // 8), F32),
+            dma((8,)), dma((8,)), dma((2,)), dma((2,)), dma((2,)), dma((2,)),
+        ],
+        compiler_params=pltpu.CompilerParams(vmem_limit_bytes=67043328),
+        cost_estimate=pl.CostEstimate(flops=20_000_000_000, bytes_accessed=70_000_000, transcendentals=0),
+        name='finish',
+    )(hid, tail, near, *factors, learn_rate)
+
+
 def solution(mesh):
     left_spec = P('pool', None, 'tp', None)
     right_spec = P('pool', None, None, 'tp')
     prompt_spec = P('pool', None, None)
 
     def local_step(base_up, base_down, up_left, up_right, down_left, down_right, grad_up_left, grad_up_right, grad_down_left, grad_down_right, learn_rate, prompts):
-        step_size = learn_rate[0]
-        t, core = lax.axis_index('tp'), lax.axis_index('pool')
+        t = lax.axis_index('tp')
         xb, yb = t % 2, t // 2
         factors = (up_left, grad_up_left, up_right, grad_up_right, down_left, grad_down_left, down_right, grad_down_right)
+        m = min(CHUNK, prompts.shape[1])
         hid, tail, near = fused_mlp(base_up, base_down, factors, learn_rate, prompts)
         from_x = lax.ppermute(tail, ('tp', 'pool'), [(2 * n, 2 * (n ^ 1) + 1) for n in range(4)])
         from_y = lax.ppermute(tail, ('tp', 'pool'), [(2 * n + 1, 2 * (n ^ 2) + 1) for n in range(4)])
-        trainer = core == 0
-        head = jnp.where(trainer, jnp.zeros_like(hid), hid)[None]
-        new = [jnp.where(trainer, value - step_size * grad, jnp.zeros_like(value))
-               for value, grad in zip(factors[::2], factors[1::2])]
-        new_up_left, new_up_right, new_down_left, new_down_right = new
-        last = jnp.concatenate([jnp.where(xb == 0, near, from_x), jnp.where(xb == 0, from_x, near),
-                                jnp.where(yb == 0, tail, from_y), jnp.where(yb == 0, from_y, tail)], axis=0)
-        last = jnp.where(trainer, jnp.zeros_like(last), last)[None]
-        head = lax.optimization_barrier(head)
-        hidden_out = lax.dynamic_update_slice(head, last, (0, hid.shape[0] - last.shape[1], 0))
+        hidden_out, new_up_left, new_up_right, new_down_left, new_down_right = finish(hid, tail, near, factors, learn_rate, m)
+        start = hid.shape[0] - m
+        hidden_out = lax.dynamic_update_slice(hidden_out, from_x[None], (0, start + (1 - xb) * (m // 4), 0))
+        hidden_out = lax.dynamic_update_slice(hidden_out, from_y[None], (0, start + m // 2 + (1 - yb) * (m // 4), 0))
         return new_up_left, new_up_right, new_down_left, new_down_right, hidden_out
 
     return jax.shard_map(local_step, mesh=mesh,

time: 552 us -> 540 us (0.978)
  other arithmetic: 41.4 us -> 0 us
  Pallas kernels: 501 us -> 525 us
    pallas_call x0 -> x1, Pallas kernels: none -> 24.1 us  [finish(): pl.pallas_call(functools.partial(finish_kernel, (tokens, d, m, step)), ou...]
    broadcast_in_dim x1 -> x0, other arithmetic: 22.9 us -> none  [local_step(): head = jnp.where(trainer, jnp.zeros_like(hid), hid)[None]]
    select_n x4 -> x0, other arithmetic: 10.8 us -> none  [local_step(): jnp.where(trainer, value - step_size * grad, jnp.zeros_like(value))]
    dynamic_update_slice x0 -> x2, local copies, waits for them, and re-layouts: none -> 6.2 us  [the longest x1 3.1 us: local_step(): lax.dynamic_update_slice(hidden_out, from_x[None], (0, start + (1 - xb) *...]
  transfers between devices with their start and end apart: 2 -> 2, of which waited for: 0 -> 0; matrix products, arithmetic and copies ran while one was open for 7% -> 1% of each run, Pallas kernels for 0% -> 4%
where the time goes in v3:
time: 540 us; the launch traced here: 538 us
  Pallas kernels  525 us (97%)
  local copies, waits for them, and re-layouts  6.2 us (1%)
  starting transfers between devices  5.75 us (1%)
    pallas_call x1, Pallas kernels, fused_mlp(): pl.pallas_call(functools.partial(mlp_kernel, dims), out_shape=(jax.ShapeD...  501 us
    pallas_call x1, Pallas kernels, finish(): pl.pallas_call(functools.partial(finish_kernel, (tokens, d, m, step)), ou...  24.1 us
  transfers between devices with their start and end apart: 2, of which 0 were waited for; matrix products, arithmetic and copies ran while one was open for 1% of the time, Pallas kernels for 4%

profile of v3, /device:TPU:1, one launch (start us, length us, event | category | flops | bytes accessed | tf_op | source)
XLA Modules:
  0.0 538.4 jit_solution(2936102066529411501)
XLA Ops:
  1.3 501.0 %mlp_ring.1 = (bf16[2048,8192]{1,0:T(8,128)(2,1)}, bf16[128,8192]{1,0:T(8,128)(2,1)}, bf16[128,8192]{1,0:T(8,128)(2,1)}, bf16[32,8192,256]{2,1,0:T(8,128)(2,1)}) custom-call(bf16[1,8192,8192]{2,1,0:T(8,128)(2,1)} %base_up.1, bf16[1,8192,8192]{2,1,0:T(8,128)(2,1)} %base_dn.1, f32[1,1,2048,128]{3,2,1,0:T(8,128)} %a_up.3, f32[1,1,2048,128]{3,2,1,0:T(8,128)} %a_up_g.3, ...), custom_call_target="tpu_custom_call" | custom-call | tf_op jit(solution)/shard_map/mlp_ring/pallas_call | solution.py:512
  502.3 1.3 collective-permute-start
  503.6 4.5 collective-permute-start.1
  508.0 24.1 %finish.1 = (bf16[1,2048,8192]{2,1,0:T(8,128)(2,1)}, f32[1,1,2048,128]{3,2,1,0:T(8,128)}, f32[1,1,128,8192]{3,2,1,0:T(8,128)}, f32[1,1,8192,128]{3,2,1,0:T(8,128)}, f32[1,1,128,2048]{3,2,1,0:T(8,128)}) custom-call(bf16[2048,8192]{1,0:T(8,128)(2,1)} %get-tuple-element.13.hid, bf16[128,8192]{1,0:T(8,128)(2,1)} %get-tuple-element.14.tail, ...), custom_call_target="tpu_custom_call" | custom-call | flops 20000000000 | bytes 70000000 | tf_op jit(solution)/shard_map/finish/pallas_call | solution.py:654
  532.2 0.0 collective-permute-done
  532.2 3.1 bitcast_dynamic-update-slice_fusion.1
  535.3 0.0 collective-permute-done.1
  535.3 3.1 bitcast_dynamic-update-slice_fusion
Async XLA Ops:
  502.3 29.9 %collective-permute-start = (bf16[128,8192]{1,0:T(8,128)(2,1)}, bf16[128,8192]{1,0:T(8,128)(2,1)}, u32[]{:S(2)}, u32[]{:S(2)}) collective-permute-start(bf16[128,8192]{1,0:T(8,128)(2,1)} %get-tuple-element.14.tail), channel_id=1, source_target_pairs={{0,3},{2,1},{4,7},{6,5}} | collective-permute-start | bytes 6291464 | tf_op jit(solution)/shard_map/ppermute | solution.py:684
  503.6 31.8 %collective-permute-start.1 = (bf16[128,8192]{1,0:T(8,128)(2,1)}, bf16[128,8192]{1,0:T(8,128)(2,1)}, u32[]{:S(2)}, u32[]{:S(2)}) collective-permute-start(bf16[128,8192]{1,0:T(8,128)(2,1)} %get-tuple-element.14.tail), channel_id=1, source_target_pairs={{1,5},{3,7},{5,1},{7,3}} | collective-permute-start | bytes 6291464 | tf_op jit(solution)/shard_map/ppermute | solution.py:685

commit v4 on v3

--- a/solution.py
+++ b/solution.py
@@ -17,8 +17,8 @@
 
 
 def mlp_kernel(dims, base_up, base_dn, a_up, a_up_g, b_up, b_up_g, a_dn, a_dn_g, b_dn, b_dn_g, rate, prompts, hid, tail, near, wm,
-               left, right, x, u, wb, aup, bup, adn, bdn, pb, rx0, s1, rx1, rx2, ob, res,
-               wsem, osem, lsem, rsem, asend, arecv, xsem, s0, r0, ss1, rs1, ss2, rs2, ss3, rs3, ss4, ss5, fsem,
+               left, right, far_a, x, u, wb, aup, bup, adn, bdn, pb, rx0, s1, rx1, rx2, ob, res,
+               wsem, osem, lsem, rsem, qload, qstore, asend, arecv, xsem, xqsem, s0, r0, ss1, rs1, ss2, rs2, ss3, rs3, ss4, ss5, fsem,
                xfree, cr1, cr2, cr3):
     m, nc, nb, d, fh, w = dims
     total = nc * nb
@@ -35,6 +35,7 @@
     b2 = c * xb + (1 - c) * yb
     p1 = (1 - c) * near_x + c * near_y
     p2 = c * near_x + (1 - c) * near_y
+    others = (near_x, near_y, 3 - t)
 
     def rows(start, size):
         return pl.ds(pl.multiple_of(start, size), size)
@@ -46,7 +47,9 @@
     def base_loads(r, slot):
         @pl.when(r < nb)
         def _():
-            pltpu.make_async_copy(base_up.at[0, :, rows(c * fh + r * TILE, TILE)], wb.at[slot], wsem.at[slot]).start()
+            for q in others:
+                pltpu.make_async_copy(base_up.at[0, rows(q * d4, d4), rows(c * fh + r * TILE, TILE)],
+                                      wb.at[slot, rows(q * d4, d4), :], wsem.at[slot]).start()
 
         @pl.when(r >= nb)
         def _():
@@ -54,26 +57,67 @@
                 pltpu.make_async_copy(base_dn.at[0, rows(c * fh, fh), rows((r - nb) * w + h * TILE, TILE)],
                                       wb.at[slot, pl.ds(h * fh, fh), :], wsem.at[slot]).start()
 
+    def up_wait(slot):
+        part = wb.at[slot, pl.ds(0, 3 * d4), :]
+        pltpu.make_async_copy(part, part, wsem.at[slot]).wait()
+
+    def up_store(r, slot):
+        for q in others:
+            pltpu.make_async_copy(wb.at[slot, rows(q * d4, d4), :], wm.at[r, rows(q * d4, d4), :], osem.at[slot]).start()
+
+    def up_store_wait(slot):
+        part = wb.at[slot, pl.ds(0, 3 * d4), :]
+        pltpu.make_async_copy(part, part, osem.at[slot]).wait()
+
     def merged_load(r, slot):
         return pltpu.make_async_copy(wm.at[r], wb.at[slot], wsem.at[slot])
 
     def merged_store(r, slot):
         return pltpu.make_async_copy(wb.at[slot], wm.at[r], osem.at[slot])
 
-    piece = min(512, fh)
+    piece = min(512, d4)
 
     def merge_up(slot, j):
-        right = bup[:, rows(j * TILE, TILE)]
-        for q in range(d // piece):
-            part = pl.ds(q * piece, piece)
-            delta = jnp.dot(aup[part, :], right, preferred_element_type=F32).astype(BF16)
-            wb[slot, part, :] = wb[slot, part, :] + delta
+        cols = bup[:, rows(j * TILE, TILE)]
+        for q in others:
+            for n in range(d4 // piece):
+                part = rows(q * d4 + n * piece, piece)
+                delta = jnp.dot(aup[part, :], cols, preferred_element_type=F32).astype(BF16)
+                wb[slot, part, :] = wb[slot, part, :] + delta
+
+    def own_rows(j):
+        return wb.at[RING - 1, rows((j % 4) * d4, d4), :]
+
+    def own_load(j):
+        return pltpu.make_async_copy(base_up.at[0, rows(t * d4, d4), rows(c * fh + j * TILE, TILE)], own_rows(j), qload.at[j % 4])
+
+    def own_store(j):
+        return pltpu.make_async_copy(own_rows(j), wm.at[j, rows(t * d4, d4), :], qstore.at[j % 4])
+
+    def own_merge(j):
+        cols = bup[:, rows(j * TILE, TILE)]
+        for n in range(d4 // piece):
+            part = rows((j % 4) * d4 + n * piece, piece)
+            delta = jnp.dot(aup[rows(t * d4 + n * piece, piece), :], cols, preferred_element_type=F32).astype(BF16)
+            wb[RING - 1, part, :] = wb[RING - 1, part, :] + delta
+
+    def own_dot(j):
+        pre = jnp.dot(x[:, rows(t * d4, d4)], wb[RING - 1, rows((j % 4) * d4, d4), :], preferred_element_type=F32)
+        s1[j, :, pl.ds(0, TILE)] = pre[:mh]
+        s1[j, :, pl.ds(TILE, TILE)] = pre[mh:]
+
+    def other_parts(slot, j):
+        pre = sum(jnp.dot(x[:, rows(q * d4, d4)], wb[slot, rows(q * d4, d4), :], preferred_element_type=F32) for q in others)
+        top = pre[:mh] + s1[j, :, pl.ds(0, TILE)]
+        low = pre[mh:] + s1[j, :, pl.ds(TILE, TILE)]
+        u[pl.ds(0, mh), rows(j * TILE, TILE)] = jax.nn.gelu(top, approximate=True).astype(BF16)
+        u[pl.ds(mh, mh), rows(j * TILE, TILE)] = jax.nn.gelu(low, approximate=True).astype(BF16)
 
     def merge_dn(slot, i):
         for h in range(halves):
-            right = bdn[:, rows(i * w + h * TILE, TILE)]
+            cols = bdn[:, rows(i * w + h * TILE, TILE)]
             for q in range(fh // piece):
-                delta = jnp.dot(adn[pl.ds(q * piece, piece), :], right, preferred_element_type=F32).astype(BF16)
+                delta = jnp.dot(adn[pl.ds(q * piece, piece), :], cols, preferred_element_type=F32).astype(BF16)
                 part = pl.ds(h * fh + q * piece, piece)
                 wb[slot, part, :] = wb[slot, part, :] + delta
 
@@ -242,8 +286,6 @@
     def dn_piece(owner):
         return bdn.at[:, rows(owner * d4, d4)]
 
-    others = (near_x, near_y, 3 - t)
-
     def up_out(n):
         return remote(up_piece(t), up_piece(t), asend.at[n], arecv.at[t], (others[n], 0))
 
@@ -263,7 +305,6 @@
         return remote(dn_piece(others[n]), dn_piece(others[n]), asend.at[11 + n], arecv.at[4 + others[n]], (t, 1))
 
     far_b = u.at[pl.ds(0, rank), :]
-    far_a = wb.at[2, pl.ds(0, fh), pl.ds(0, rank)]
     own = (
         lambda: remote(up_piece(t), up_piece(t), asend.at[14], arecv.at[t], (t, 1)),
         lambda: remote(far_b, bup, asend.at[15], arecv.at[8], (t, 1)),
@@ -274,7 +315,7 @@
     size = d4 // 2
     lefts = [(a_up, a_up_g, q, aup, t * d4 + q * size) for q in range(2)]
     lefts += [(a_dn, a_dn_g, q, adn, q * size) for q in range(4)]
-    lefts += [(a_dn, a_dn_g, 4 + q, None, q * size) for q in range(4)]
+    lefts += [(a_dn, a_dn_g, 4 + q, far_a, q * size) for q in range(4)]
     rights = [(b_up, b_up_g, q, bup, q * size) for q in range(4)]
     rights += [(b_up, b_up_g, 4 + q, u, q * size) for q in range(4)]
     rights += [(b_dn, b_dn_g, q, bdn, t * d4 + q * size) for q in range(2)]
@@ -293,10 +334,7 @@
         _, _, _, dst, start = lefts[n]
         pltpu.make_async_copy(left.at[n % 2], left.at[n % 2], lsem.at[n % 2]).wait()
         new = (left[n % 2, 0] - rate[0] * left[n % 2, 1]).astype(BF16)
-        if dst is None:
-            wb[2, rows(start, size), pl.ds(0, rank)] = new
-        else:
-            dst[rows(start, size), :] = new
+        dst[rows(start, size), :] = new
         if n + 2 < len(lefts):
             left_load(n + 2)
 
@@ -311,14 +349,26 @@
         if n + 2 < len(rights):
             right_load(n + 2)
 
+    def x_quarter(owner):
+        return pltpu.make_async_copy(prompts.at[0, pl.ds(0, m), rows(owner * d4, d4)], x.at[:, rows(owner * d4, d4)],
+                                     xqsem.at[0 if owner is t else 1])
+
+    def x_quarter_send(owner):
+        part = x.at[:, rows(owner * d4, d4)]
+        return remote(part, part, xqsem.at[2 if owner is t else 3], xqsem.at[4 if owner is t else 5], (t, 0))
+
+    def three(sem):
+        part = x.at[:, pl.ds(0, 3 * d4)]
+        return pltpu.make_async_copy(part, part, sem)
+
     @pl.when(c == 0)
     def _():
         for n in range(2):
             left_load(n)
         for n in range(2):
             right_load(n)
-        base_loads(0, 0)
-        base_loads(1, 1)
+        for n in range(2):
+            own_load(n).start()
         for n in range(2):
             left_update(n)
         for n in range(3):
@@ -327,40 +377,93 @@
         for n in range(8):
             right_update(n)
         own[1]().start()
-        for n in range(8, 10):
-            right_update(n)
-        for n in range(3):
-            dn_out(n).start()
-        own[3]().start()
-        for n in range(2, 10):
-            left_update(n)
-        own[2]().start()
-        for n in range(3):
-            up_in(others[n]).wait_recv()
-            pass_up(n).start()
-        own[1]().wait_send()
-        own[2]().wait_send()
-        x_send().wait_recv()
+        base_loads(0, 0)
+        base_loads(1, 1)
+        x_quarter_send(t).wait_recv()
 
     @pl.when(c == 1)
     def _():
-        x_load(0).start()
+        x_quarter(t).start()
+        for owner in others:
+            x_quarter(owner).start()
+        for n in range(2):
+            own_load(n).start()
         base_loads(0, 0)
         base_loads(1, 1)
-        x_load(0).wait()
-        x_send().start()
-        for owner in range(4):
+        x_quarter(t).wait()
+        x_quarter_send(t).start()
+        three(xqsem.at[1]).wait()
+        for owner in others:
+            x_quarter_send(owner).start()
+        up_in(t).wait_recv()
+        own[1]().wait_recv()
+
+    own_load(0).wait()
+    own_merge(0)
+    own_store(0).start()
+
+    def first_part(j, carry):
+        @pl.when(j >= 2)
+        def _():
+            own_store(j - 2).wait()
+
+        @pl.when(j + 2 < nb)
+        def _():
+            own_load(j + 2).start()
+        own_load(j + 1).wait()
+        own_dot(j)
+        own_merge(j + 1)
+        own_store(j + 1).start()
+
+        def turn(n, *calls):
+            @pl.when((c == 0) & (j == n * nb // 16))
+            def _():
+                for call in calls:
+                    call()
+
+        for n in range(2):
+            turn(1 + n, functools.partial(right_update, 8 + n))
+        turn(3, *[lambda n=n: dn_out(n).start() for n in range(3)], lambda: own[3]().start())
+        for n in range(4):
+            turn(4 + n, functools.partial(left_update, 2 + 2 * n), functools.partial(left_update, 3 + 2 * n))
+        turn(8, lambda: own[2]().start())
+        for n in range(3):
+            turn((9, 10, 14)[n], lambda n=n: up_in(others[n]).wait_recv(), lambda n=n: pass_up(n).start())
+        return carry
+
+    lax.fori_loop(0, nb - 1, first_part, 0)
+    own_dot(nb - 1)
+    for j in range(nb - 3, nb):
+        own_store(j).wait()
+
+    @pl.when(c == 0)
+    def _():
+        own[1]().wait_send()
+        three(xqsem.at[5]).wait()
+
+    @pl.when(c == 1)
+    def _():
+        for owner in others:
             up_in(owner).wait_recv()
-        own[1]().wait_recv()
-
-    merged_load(0, 0).wait()
+
+    up_wait(0)
     merge_up(0, 0)
     keep_rows(0)
 
     def tile_turn(r):
-        merged_store(r, r % RING).start()
-
-        @pl.when(r >= 1)
+        @pl.when(r < nb)
+        def _():
+            up_store(r, r % RING)
+
+        @pl.when(r >= nb)
+        def _():
+            merged_store(r, r % RING).start()
+
+        @pl.when((r >= 1) & (r <= nb))
+        def _():
+            up_store_wait((r + 2) % RING)
+
+        @pl.when(r > nb)
         def _():
             merged_store(r - 1, (r + 2) % RING).wait()
 
@@ -372,7 +475,13 @@
         def _():
             merged_load(r + 2 - 2 * nb, (r + 2) % RING).start()
 
-        merged_load(0, (r + 1) % RING).wait()
+        @pl.when(r + 1 < nb)
+        def _():
+            up_wait((r + 1) % RING)
+
+        @pl.when(r + 1 >= nb)
+        def _():
+            merged_load(0, (r + 1) % RING).wait()
 
     def first_up(r, carry):
         @pl.when(r == nb // 2)
@@ -383,11 +492,8 @@
                     dn_in(others[n]).wait_recv()
                     pass_dn(n).start()
         tile_turn(r)
-        dot_up(r % RING, r)
-
-        @pl.when(r < nb)
-        def _():
-            merge_up((r + 1) % RING, r + 1)
+        other_parts(r % RING, r)
+        merge_up((r + 1) % RING, r + 1)
         return carry
 
     lax.fori_loop(0, nb - 1, first_up, 0)
@@ -399,8 +505,8 @@
             dn_out(n).wait_send()
             pass_up(n).wait_send()
             pass_dn(n).wait_send()
-        own[0]().wait_send()
-        own[3]().wait_send()
+        for n in (0, 2, 3):
+            own[n]().wait_send()
 
     @pl.when(c == 1)
     def _():
@@ -409,8 +515,8 @@
         own[2]().wait_recv()
 
     tile_turn(nb - 1)
+    other_parts((nb - 1) % RING, nb - 1)
     merge_dn(nb % RING, 0)
-    dot_up((nb - 1) % RING, nb - 1)
 
     def x_turn(k, r):
         @pl.when((k + 1 < nc) & (c == 0) & (r == nb))
@@ -419,7 +525,12 @@
 
         @pl.when((k + 1 < nc) & (c == 1) & (r == nb))
         def _():
-            @pl.when(k >= 0)
+            @pl.when(k == 0)
+            def _():
+                x_quarter_send(t).wait_send()
+                three(xqsem.at[3]).wait()
+
+            @pl.when(k >= 1)
             def _():
                 x_send().wait_send()
             x_load(k + 1).start()
@@ -518,6 +629,7 @@
         scratch_shapes=[
             pltpu.VMEM((2, 2, d // 8, rank), F32),
             pltpu.VMEM((2, 2, rank, d // 8), F32),
+            pltpu.VMEM((fh, rank), BF16),
             pltpu.VMEM((m, d), BF16),
             pltpu.VMEM((m, fh), BF16),
             pltpu.VMEM((RING, d, TILE), BF16),
@@ -532,7 +644,7 @@
             pltpu.VMEM((nb, m // 8, w), F32),
             pltpu.VMEM((nb, m // 4, w), BF16),
             pltpu.VMEM((2, m // 8, d), BF16),
-            dma((RING,)), dma((RING,)), dma((2,)), dma((2,)), dma((18,)), dma((10,)), dma((3,)),
+            dma((RING,)), dma((RING,)), dma((2,)), dma((2,)), dma((4,)), dma((4,)), dma((18,)), dma((10,)), dma((3,)), dma((6,)),
             dma((2,)), dma((4,)), dma((nb,)), dma((nb,)), dma((nb,)), dma((nb,)), dma((nb,)), dma((nb,)),
             dma((nb,)), dma((nb,)), dma((4,)),
             pltpu.SemaphoreType.REGULAR, pltpu.SemaphoreType.REGULAR,

time: 540 us -> 540 us (level)
  no operation moved by 1% of the time
where the time goes in v4:
time: 540 us
  Pallas kernels  527 us (98%)
  local copies, waits for them, and re-layouts  6.2 us (1%)
    pallas_call x1, Pallas kernels, fused_mlp(): pl.pallas_call(functools.partial(mlp_kernel, dims), out_shape=(jax.ShapeD...  503 us
    pallas_call x1, Pallas kernels, finish(): pl.pallas_call(functools.partial(finish_kernel, (tokens, d, m, step)), ou...  24.1 us
  transfers between devices with their start and end apart: 2, of which 0 were waited for; matrix products, arithmetic and copies ran while one was open for 1% of the time, Pallas kernels for 4%

profile of v4, /device:TPU:1, one launch (start us, length us, event | category | flops | bytes accessed | tf_op | source)
XLA Modules:
  0.0 539.7 jit_solution(3964974097666483346)
XLA Ops:
  1.3 503.3 %mlp_ring.1 = (bf16[2048,8192]{1,0:T(8,128)(2,1)}, bf16[128,8192]{1,0:T(8,128)(2,1)}, bf16[128,8192]{1,0:T(8,128)(2,1)}, bf16[32,8192,256]{2,1,0:T(8,128)(2,1)}) custom-call(bf16[1,8192,8192]{2,1,0:T(8,128)(2,1)} %base_up.1, bf16[1,8192,8192]{2,1,0:T(8,128)(2,1)} %base_dn.1, f32[1,1,2048,128]{3,2,1,0:T(8,128)} %a_up.3, f32[1,1,2048,128]{3,2,1,0:T(8,128)} %a_up_g.3, ...), custom_call_target="tpu_custom_call" | custom-call | tf_op jit(solution)/shard_map/mlp_ring/pallas_call | solution.py:623
  504.5 1.3 collective-permute-start
  505.8 3.5 collective-permute-start.1
  509.3 24.1 %finish.1 = (bf16[1,2048,8192]{2,1,0:T(8,128)(2,1)}, f32[1,1,2048,128]{3,2,1,0:T(8,128)}, f32[1,1,128,8192]{3,2,1,0:T(8,128)}, f32[1,1,8192,128]{3,2,1,0:T(8,128)}, f32[1,1,128,2048]{3,2,1,0:T(8,128)}) custom-call(bf16[2048,8192]{1,0:T(8,128)(2,1)} %get-tuple-element.13.hid, bf16[128,8192]{1,0:T(8,128)(2,1)} %get-tuple-element.14.tail, ...), custom_call_target="tpu_custom_call" | custom-call | flops 20000000000 | bytes 70000000 | tf_op jit(solution)/shard_map/finish/pallas_call | solution.py:766
  533.5 0.0 collective-permute-done
  533.5 3.1 bitcast_dynamic-update-slice_fusion.1
  536.6 0.0 collective-permute-done.1
  536.6 3.1 bitcast_dynamic-update-slice_fusion
Async XLA Ops:
  504.5 29.0 %collective-permute-start = (bf16[128,8192]{1,0:T(8,128)(2,1)}, bf16[128,8192]{1,0:T(8,128)(2,1)}, u32[]{:S(2)}, u32[]{:S(2)}) collective-permute-start(bf16[128,8192]{1,0:T(8,128)(2,1)} %get-tuple-element.14.tail), channel_id=1, source_target_pairs={{0,3},{2,1},{4,7},{6,5}} | collective-permute-start | bytes 6291464 | tf_op jit(solution)/shard_map/ppermute | solution.py:796
  505.8 30.8 %collective-permute-start.1 = (bf16[128,8192]{1,0:T(8,128)(2,1)}, bf16[128,8192]{1,0:T(8,128)(2,1)}, u32[]{:S(2)}, u32[]{:S(2)}) collective-permute-start(bf16[128,8192]{1,0:T(8,128)(2,1)} %get-tuple-element.14.tail), channel_id=1, source_target_pairs={{1,5},{3,7},{5,1},{7,3}} | collective-permute-start | bytes 6291464 | tf_op jit(solution)/shard_map/ppermute | solution.py:797

commit v5 on v4

--- a/solution.py
+++ b/solution.py
@@ -10,6 +10,7 @@
 CHUNK = 512
 TILE = 256
 RING = 3
+PIECE = 1024
 LAG = (2, 4, 7, 23)
 BF16 = jnp.bfloat16
 F32 = jnp.float32
@@ -29,6 +30,8 @@
     rank = aup.shape[1]
     t = lax.axis_index('tp')
     c = lax.axis_index('pool')
+    trainer, generator = c == 0, c == 1
+    period = 2 * nb
     xb, yb = t % 2, t // 2
     near_x, near_y = t + 1 - 2 * xb, t + 2 - 4 * yb
     b1 = (1 - c) * xb + c * yb
@@ -44,18 +47,23 @@
         return pltpu.make_async_remote_copy(src_ref=src, dst_ref=dst, send_sem=send, recv_sem=recv,
                                             device_id=device, device_id_type=MESH)
 
+    def spread(src, dst, sem):
+        size = min(PIECE, src.shape[0])
+        for start in range(0, src.shape[0], size):
+            pltpu.make_async_copy(src.at[pl.ds(start, size)], dst.at[pl.ds(start, size)], sem).start()
+
     def base_loads(r, slot):
         @pl.when(r < nb)
         def _():
             for q in others:
-                pltpu.make_async_copy(base_up.at[0, rows(q * d4, d4), rows(c * fh + r * TILE, TILE)],
-                                      wb.at[slot, rows(q * d4, d4), :], wsem.at[slot]).start()
+                spread(base_up.at[0, rows(q * d4, d4), rows(c * fh + r * TILE, TILE)],
+                       wb.at[slot, rows(q * d4, d4), :], wsem.at[slot])
 
         @pl.when(r >= nb)
         def _():
             for h in range(halves):
-                pltpu.make_async_copy(base_dn.at[0, rows(c * fh, fh), rows((r - nb) * w + h * TILE, TILE)],
-                                      wb.at[slot, pl.ds(h * fh, fh), :], wsem.at[slot]).start()
+                spread(base_dn.at[0, rows(c * fh, fh), rows((r - nb) * w + h * TILE, TILE)],
+                       wb.at[slot, pl.ds(h * fh, fh), :], wsem.at[slot])
 
     def up_wait(slot):
         part = wb.at[slot, pl.ds(0, 3 * d4), :]
@@ -63,7 +71,7 @@
 
     def up_store(r, slot):
         for q in others:
-            pltpu.make_async_copy(wb.at[slot, rows(q * d4, d4), :], wm.at[r, rows(q * d4, d4), :], osem.at[slot]).start()
+            spread(wb.at[slot, rows(q * d4, d4), :], wm.at[r, rows(q * d4, d4), :], osem.at[slot])
 
     def up_store_wait(slot):
         part = wb.at[slot, pl.ds(0, 3 * d4), :]
@@ -89,10 +97,13 @@
         return wb.at[RING - 1, rows((j % 4) * d4, d4), :]
 
     def own_load(j):
-        return pltpu.make_async_copy(base_up.at[0, rows(t * d4, d4), rows(c * fh + j * TILE, TILE)], own_rows(j), qload.at[j % 4])
+        spread(base_up.at[0, rows(t * d4, d4), rows(c * fh + j * TILE, TILE)], own_rows(j), qload.at[j % 4])
 
     def own_store(j):
-        return pltpu.make_async_copy(own_rows(j), wm.at[j, rows(t * d4, d4), :], qstore.at[j % 4])
+        spread(own_rows(j), wm.at[j, rows(t * d4, d4), :], qstore.at[j % 4])
+
+    def own_wait(j, sem):
+        pltpu.make_async_copy(own_rows(j), own_rows(j), sem.at[j % 4]).wait()
 
     def own_merge(j):
         cols = bup[:, rows(j * TILE, TILE)]
@@ -214,11 +225,11 @@
         def _():
             final_far(g).start()
 
-            @pl.when(c == 0)
+            @pl.when(trainer)
             def _():
                 final_near(g).start()
 
-            @pl.when(c == 1)
+            @pl.when(generator)
             def _():
                 final_local(g).start()
 
@@ -226,7 +237,7 @@
         def _():
             tail_local(g).start()
 
-            @pl.when(c == 0)
+            @pl.when(trainer)
             def _():
                 tail_near(g).start()
 
@@ -237,11 +248,11 @@
         def _():
             final_far(g).wait_send()
 
-            @pl.when(c == 0)
+            @pl.when(trainer)
             def _():
                 final_near(g).wait_send()
 
-            @pl.when(c == 1)
+            @pl.when(generator)
             def _():
                 final_local(g).wait()
 
@@ -249,7 +260,7 @@
         def _():
             tail_local(g).wait()
 
-            @pl.when(c == 0)
+            @pl.when(trainer)
             def _():
                 tail_near(g).wait_send()
 
@@ -259,11 +270,11 @@
 
     def stages(s):
         before = s - 1
-        r = before % (2 * nb)
-
-        @pl.when((r >= nb) & (before < 2 * nb * nc))
-        def _():
-            stage_a((before // (2 * nb)) * nb + r - nb)
+        r = before % period
+
+        @pl.when((r >= nb) & (before < period * nc))
+        def _():
+            stage_a((before // period) * nb + r - nb)
         for lag, stage in zip(LAG, (stage_b, stage_c, stage_d, stage_e)):
             late = s - nb - lag
 
@@ -361,14 +372,14 @@
         part = x.at[:, pl.ds(0, 3 * d4)]
         return pltpu.make_async_copy(part, part, sem)
 
-    @pl.when(c == 0)
+    @pl.when(trainer)
     def _():
         for n in range(2):
             left_load(n)
         for n in range(2):
             right_load(n)
         for n in range(2):
-            own_load(n).start()
+            own_load(n)
         for n in range(2):
             left_update(n)
         for n in range(3):
@@ -381,13 +392,13 @@
         base_loads(1, 1)
         x_quarter_send(t).wait_recv()
 
-    @pl.when(c == 1)
+    @pl.when(generator)
     def _():
         x_quarter(t).start()
         for owner in others:
             x_quarter(owner).start()
         for n in range(2):
-            own_load(n).start()
+            own_load(n)
         base_loads(0, 0)
         base_loads(1, 1)
         x_quarter(t).wait()
@@ -398,25 +409,25 @@
         up_in(t).wait_recv()
         own[1]().wait_recv()
 
-    own_load(0).wait()
+    own_wait(0, qload)
     own_merge(0)
-    own_store(0).start()
+    own_store(0)
 
     def first_part(j, carry):
         @pl.when(j >= 2)
         def _():
-            own_store(j - 2).wait()
+            own_wait(j - 2, qstore)
 
         @pl.when(j + 2 < nb)
         def _():
-            own_load(j + 2).start()
-        own_load(j + 1).wait()
+            own_load(j + 2)
+        own_wait(j + 1, qload)
         own_dot(j)
         own_merge(j + 1)
-        own_store(j + 1).start()
+        own_store(j + 1)
 
         def turn(n, *calls):
-            @pl.when((c == 0) & (j == n * nb // 16))
+            @pl.when((trainer) & (j == n * (nb - 1) // 16))
             def _():
                 for call in calls:
                     call()
@@ -434,14 +445,14 @@
     lax.fori_loop(0, nb - 1, first_part, 0)
     own_dot(nb - 1)
     for j in range(nb - 3, nb):
-        own_store(j).wait()
-
-    @pl.when(c == 0)
+        own_wait(j, qstore)
+
+    @pl.when(trainer)
     def _():
         own[1]().wait_send()
         three(xqsem.at[5]).wait()
 
-    @pl.when(c == 1)
+    @pl.when(generator)
     def _():
         for owner in others:
             up_in(owner).wait_recv()
@@ -457,7 +468,7 @@
 
         @pl.when(r >= nb)
         def _():
-            merged_store(r, r % RING).start()
+            spread(wb.at[r % RING], wm.at[r], osem.at[r % RING])
 
         @pl.when((r >= 1) & (r <= nb))
         def _():
@@ -467,13 +478,13 @@
         def _():
             merged_store(r - 1, (r + 2) % RING).wait()
 
-        @pl.when(r + 2 < 2 * nb)
+        @pl.when(r + 2 < period)
         def _():
             base_loads(r + 2, (r + 2) % RING)
 
-        @pl.when(r + 2 >= 2 * nb)
-        def _():
-            merged_load(r + 2 - 2 * nb, (r + 2) % RING).start()
+        @pl.when(r + 2 >= period)
+        def _():
+            spread(wm.at[r + 2 - period], wb.at[(r + 2) % RING], wsem.at[(r + 2) % RING])
 
         @pl.when(r + 1 < nb)
         def _():
@@ -486,7 +497,7 @@
     def first_up(r, carry):
         @pl.when(r == nb // 2)
         def _():
-            @pl.when(c == 0)
+            @pl.when(trainer)
             def _():
                 for n in range(3):
                     dn_in(others[n]).wait_recv()
@@ -498,7 +509,7 @@
 
     lax.fori_loop(0, nb - 1, first_up, 0)
 
-    @pl.when(c == 0)
+    @pl.when(trainer)
     def _():
         for n in range(3):
             up_out(n).wait_send()
@@ -508,7 +519,7 @@
         for n in (0, 2, 3):
             own[n]().wait_send()
 
-    @pl.when(c == 1)
+    @pl.when(generator)
     def _():
         for owner in range(4):
             dn_in(owner).wait_recv()
@@ -519,11 +530,11 @@
     merge_dn(nb % RING, 0)
 
     def x_turn(k, r):
-        @pl.when((k + 1 < nc) & (c == 0) & (r == nb))
+        @pl.when((k + 1 < nc) & (trainer) & (r == nb))
         def _():
             pl.semaphore_signal(xfree, inc=1, device_id=(t, 1), device_id_type=MESH)
 
-        @pl.when((k + 1 < nc) & (c == 1) & (r == nb))
+        @pl.when((k + 1 < nc) & (generator) & (r == nb))
         def _():
             @pl.when(k == 0)
             def _():
@@ -535,7 +546,7 @@
                 x_send().wait_send()
             x_load(k + 1).start()
 
-        @pl.when((k + 1 < nc) & (c == 1) & (r == nb + 2))
+        @pl.when((k + 1 < nc) & (generator) & (r == nb + 2))
         def _():
             x_load(k + 1).wait()
             pl.semaphore_wait(xfree, 1)
@@ -543,7 +554,7 @@
 
         @pl.when((k >= 1) & (r == 0))
         def _():
-            @pl.when(c == 0)
+            @pl.when(trainer)
             def _():
                 x_send().wait_recv()
             keep_rows(k)
@@ -557,27 +568,27 @@
         stages(r)
         return carry
 
-    lax.fori_loop(nb, 2 * nb - 1, first_dn, 0)
+    lax.fori_loop(nb, period - 1, first_dn, 0)
 
     def step(s, carry):
-        k, r = s // (2 * nb), s % (2 * nb)
+        k, r = s // period, s % period
         x_turn(k, r)
 
-        @pl.when(s == 2 * nb - 1)
-        def _():
-            tile_turn(2 * nb - 1)
-
-        @pl.when(s == 2 * nb)
-        def _():
-            merged_store(2 * nb - 1, (2 * nb - 1) % RING).wait()
-
-        @pl.when(s >= 2 * nb)
-        def _():
-            @pl.when(s + 2 < 2 * nb * nc)
-            def _():
-                merged_load((s + 2) % (2 * nb), (s + 2) % RING).start()
-
-            @pl.when(s > 2 * nb)
+        @pl.when(s == period - 1)
+        def _():
+            tile_turn(period - 1)
+
+        @pl.when(s == period)
+        def _():
+            merged_store(period - 1, (period - 1) % RING).wait()
+
+        @pl.when(s >= period)
+        def _():
+            @pl.when(s + 2 < period * nc)
+            def _():
+                spread(wm.at[(s + 2) % period], wb.at[(s + 2) % RING], wsem.at[(s + 2) % RING])
+
+            @pl.when(s > period)
             def _():
                 merged_load(0, s % RING).wait()
 
@@ -592,15 +603,15 @@
         stages(s)
         return carry
 
-    lax.fori_loop(2 * nb - 1, 2 * nb * nc, step, 0)
+    lax.fori_loop(period - 1, period * nc, step, 0)
 
     def drain(s, carry):
         stages(s)
         return carry
 
-    lax.fori_loop(2 * nb * nc, 2 * (total - 1) + nb + LAG[-1] + 1, drain, 0)
-
-    @pl.when(c == 1)
+    lax.fori_loop(period * nc, 2 * (total - 1) + nb + LAG[-1] + 1, drain, 0)
+
+    @pl.when(generator)
     def _():
         x_send().wait_send()
         for n in range(3):
@@ -704,7 +715,7 @@
         for n in range(len(moves)):
             load(n).wait()
             store(n).start()
-            if n < 10:
+            if n < len(lefts):
                 left_store(n, 0).start()
                 right_store(n, 0).start()
             if n >= ahead:
@@ -713,7 +724,7 @@
                 load(n + ahead).start()
         for n in range(len(moves) - ahead, len(moves)):
             store(n).wait()
-        for n in range(10):
+        for n in range(len(lefts)):
             left_store(n, 0).wait()
             right_store(n, 0).wait()
 

time: 540 us -> 540 us (level)
  no operation moved by 1% of the time
where the time goes in v5:
time: 540 us; the launch traced here: 539 us
  Pallas kernels  527 us (98%)
  local copies, waits for them, and re-layouts  6.2 us (1%)
    pallas_call x1, Pallas kernels, fused_mlp(): pl.pallas_call(functools.partial(mlp_kernel, dims), out_shape=(jax.ShapeD...  502 us
    pallas_call x1, Pallas kernels, finish(): pl.pallas_call(functools.partial(finish_kernel, (tokens, d, m, step)), ou...  24.1 us
  transfers between devices with their start and end apart: 2, of which 0 were waited for; matrix products, arithmetic and copies ran while one was open for 1% of the time, Pallas kernels for 4%

profile of v5, /device:TPU:1, one launch (start us, length us, event | category | flops | bytes accessed | tf_op | source)
XLA Modules:
  0.0 539.2 jit_solution(16201020223198219006)
XLA Ops:
  1.3 502.5 %mlp_ring.1 = (bf16[2048,8192]{1,0:T(8,128)(2,1)}, bf16[128,8192]{1,0:T(8,128)(2,1)}, bf16[128,8192]{1,0:T(8,128)(2,1)}, bf16[32,8192,256]{2,1,0:T(8,128)(2,1)}) custom-call(bf16[1,8192,8192]{2,1,0:T(8,128)(2,1)} %base_up.1, bf16[1,8192,8192]{2,1,0:T(8,128)(2,1)} %base_dn.1, f32[1,1,2048,128]{3,2,1,0:T(8,128)} %a_up.3, f32[1,1,2048,128]{3,2,1,0:T(8,128)} %a_up_g.3, ...), custom_call_target="tpu_custom_call" | custom-call | tf_op jit(solution)/shard_map/mlp_ring/pallas_call | solution.py:634
  503.8 1.3 collective-permute-start
  505.1 3.7 collective-permute-start.1
  508.8 24.1 %finish.1 = (bf16[1,2048,8192]{2,1,0:T(8,128)(2,1)}, f32[1,1,2048,128]{3,2,1,0:T(8,128)}, f32[1,1,128,8192]{3,2,1,0:T(8,128)}, f32[1,1,8192,128]{3,2,1,0:T(8,128)}, f32[1,1,128,2048]{3,2,1,0:T(8,128)}) custom-call(bf16[2048,8192]{1,0:T(8,128)(2,1)} %get-tuple-element.13.hid, bf16[128,8192]{1,0:T(8,128)(2,1)} %get-tuple-element.14.tail, ...), custom_call_target="tpu_custom_call" | custom-call | flops 20000000000 | bytes 70000000 | tf_op jit(solution)/shard_map/finish/pallas_call | solution.py:777
  532.9 0.0 collective-permute-done
  533.0 3.1 bitcast_dynamic-update-slice_fusion.1
  536.1 0.0 collective-permute-done.1
  536.1 3.1 bitcast_dynamic-update-slice_fusion
Async XLA Ops:
  503.8 29.2 %collective-permute-start = (bf16[128,8192]{1,0:T(8,128)(2,1)}, bf16[128,8192]{1,0:T(8,128)(2,1)}, u32[]{:S(2)}, u32[]{:S(2)}) collective-permute-start(bf16[128,8192]{1,0:T(8,128)(2,1)} %get-tuple-element.14.tail), channel_id=1, source_target_pairs={{0,3},{2,1},{4,7},{6,5}} | collective-permute-start | bytes 6291464 | tf_op jit(solution)/shard_map/ppermute | solution.py:807
  505.1 31.0 %collective-permute-start.1 = (bf16[128,8192]{1,0:T(8,128)(2,1)}, bf16[128,8192]{1,0:T(8,128)(2,1)}, u32[]{:S(2)}, u32[]{:S(2)}) collective-permute-start(bf16[128,8192]{1,0:T(8,128)(2,1)} %get-tuple-element.14.tail), channel_id=1, source_target_pairs={{1,5},{3,7},{5,1},{7,3}} | collective-permute-start | bytes 6291464 | tf_op jit(solution)/shard_map/ppermute | solution.py:808
